TPU v7x, 256 devices: a 8x8x2 block of a 8x8x16 slice. The times are simulated.
256 devices in a mesh: cfg: 2 (over z), ta: 128 (over y, x, core).
Axes of the slice: x: 8, y: 8, z: 2, core: 2. Of those that a mesh axis runs over, the one named last changes fastest.
The devices are a block of a 8x8x16 slice.
Arguments:
- fine_source: bfloat16 [256, 128, 2, 2, 24, 128], P('cfg', 'ta'), parts along dimension 0, may hold values from -24 to 24
- projectors: bfloat16 [256, 128, 2304], P(('cfg', 'ta')), parts along dimension 0, may hold values from -0.21875 to 0.21875
- stencil_links: bfloat16 [256, 8, 48, 864], P(('cfg', 'ta')), parts along dimension 0, may hold values from -0.21875 to 0.21875
- quark_mass: float32 [2], P('cfg'), parts along dimension 0, may hold values from 1.5 to 3
Outputs:
- solution: float32 [256, 8, 96, 128], P(('cfg', 'ta')), parts along dimension 0
- residual: float32 [256, 8, 96, 128], P(('cfg', 'ta')), parts along dimension 0
There are 2 independent parts, one for each index of `cfg`. A program takes and returns all parts, laid end to end along the dimension named above; each array names one. Nothing has to cross between parts.
All inputs are finite; a program needn't handle non-finite values.
Results may differ from a plain program's by a relative error of at most 0.012.
The roundings to bfloat16 on the way count: a program that leaves them out, or rounds other values in their place, can miss the bound.
Values may be sent and summed in bfloat16 or wider, within the bound.
A program may use at most 128 MiB of HBM per device.

v0:
```python
import jax
import jax.numpy as jnp
from jax import lax
from jax.sharding import Mesh
from jax.sharding import PartitionSpec as P

LX = 4
LZ = 8
ITERS = 3
TA = ("ta_0", "ta_1", "ta_2")
CFG_TA = ("cfg", "ta_0", "ta_1", "ta_2")


def from_behind(value, axis, steps):
    count = lax.axis_size(axis)
    pairs = [(source, (source + steps) % count) for source in range(count)]
    return lax.ppermute(value, axis, pairs)


def by_axis(array, axes):
    for axis in axes:
        array = lax.psum(array, axis)
    return array


def real_weights(proj_view):
    proj_re = proj_view[..., 0, :]
    proj_im = proj_view[..., 1, :]
    first_row = jnp.stack([proj_re, proj_im], axis=-4)
    second_row = jnp.stack([-proj_im, proj_re], axis=-4)
    return jnp.stack([first_row, second_row], axis=-5)


def inner_local(left, right, comp_count):
    left_re = left[:, :comp_count]
    left_im = left[:, comp_count:]
    right_re = right[:, :comp_count]
    right_im = right[:, comp_count:]
    return (
        jnp.sum(left_re * right_re + left_im * right_im, axis=(0, 1)),
        jnp.sum(left_re * right_im - left_im * right_re, axis=(0, 1)),
    )


def scaled(vector, factor_re, factor_im, comp_count):
    vector_re = vector[:, :comp_count]
    vector_im = vector[:, comp_count:]
    return jnp.concatenate(
        [
            factor_re * vector_re - factor_im * vector_im,
            factor_re * vector_im + factor_im * vector_re,
        ],
        axis=1,
    )


def shards(fine_source, projectors, stencil_links, quark_mass):
    comp_count = stencil_links.shape[2]
    null_count = comp_count // 2
    site_count = stencil_links.shape[1]
    column_count = projectors.shape[1]
    block_count = column_count // site_count
    fine_count = fine_source.shape[4]
    rhs_count = fine_source.shape[5]
    regrouped = lax.all_to_all(fine_source, TA, split_axis=0, concat_axis=1, tiled=True)
    fine_local = regrouped.reshape(site_count, block_count, 2, 2, fine_count, rhs_count)
    weights = real_weights(
        projectors.reshape(site_count, block_count, 2, null_count, 2, fine_count)
    )
    source = jnp.einsum(
        "sodchvk,sochkr->sdhvr", weights, fine_local, preferred_element_type=jnp.float32
    )
    source = source.reshape(site_count, 2 * comp_count, rhs_count)
    link_view = stencil_links.reshape(site_count, comp_count, 9, 2, comp_count)
    link_re = link_view[:, :, :, 0, :]
    link_im = link_view[:, :, :, 1, :]
    upper_rows = jnp.stack([link_re, -link_im], axis=3)
    lower_rows = jnp.stack([link_im, link_re], axis=3)
    real_operator = jnp.stack([upper_rows, lower_rows], axis=1).reshape(
        site_count, 2 * comp_count, 18 * comp_count
    )
    mass_value = quark_mass[0]
    z_position = lax.axis_index(TA) % LZ
    line_count = site_count // LX

    def flatten_sites(shifted):
        return shifted.reshape(site_count, 2 * comp_count, rhs_count)

    solution = jnp.zeros_like(source)
    residual = source
    basis_q = []
    basis_p = []
    for iteration in range(ITERS):
        direction = residual
        rounded = residual.astype(jnp.bfloat16)
        plane_view = rounded.reshape(line_count, LX, 2 * comp_count, rhs_count)
        x_plus = flatten_sites(jnp.roll(plane_view, -1, axis=1))
        x_minus = flatten_sites(jnp.roll(plane_view, 1, axis=1))
        y_plus = flatten_sites(jnp.roll(plane_view, -1, axis=0))
        y_minus = flatten_sites(jnp.roll(plane_view, 1, axis=0))
        z_plus_near = from_behind(rounded, TA, -1)
        z_minus_near = from_behind(rounded, TA, 1)
        upper_pair = from_behind(jnp.stack([rounded, z_minus_near], axis=0), TA, -LZ)
        lower_pair = from_behind(jnp.stack([rounded, z_plus_near], axis=0), TA, LZ)
        t_plus = upper_pair[0]
        t_minus = lower_pair[0]
        z_plus = jnp.where(z_position == LZ - 1, lower_pair[1], z_plus_near)
        z_minus = jnp.where(z_position == 0, upper_pair[1], z_minus_near)
        stacked = jnp.stack(
            [rounded, x_plus, x_minus, y_plus, y_minus, z_plus, z_minus, t_plus, t_minus], axis=1
        )
        stacked = stacked.reshape(site_count, 18 * comp_count, rhs_count)
        product = jnp.einsum(
            "sij,sjr->sir", real_operator, stacked, preferred_element_type=jnp.float32
        )
        mapped = product + mass_value * rounded.astype(jnp.float32)
        square_loc = inner_local(mapped, mapped, comp_count)[0]
        cross_re, cross_im = inner_local(mapped, residual, comp_count)
        if iteration > 0:
            coef_pairs = [inner_local(earlier, mapped, comp_count) for earlier in basis_q]
            back_pairs = [inner_local(earlier, residual, comp_count) for earlier in basis_q]
            coef_re = jnp.stack([pair[0] for pair in coef_pairs])
            coef_im = jnp.stack([pair[1] for pair in coef_pairs])
            back_re = jnp.stack([pair[0] for pair in back_pairs])
            back_im = jnp.stack([pair[1] for pair in back_pairs])
        else:
            coef_re = jnp.zeros((1, rhs_count), jnp.float32)
            coef_im = jnp.zeros((1, rhs_count), jnp.float32)
            back_re = jnp.zeros((1, rhs_count), jnp.float32)
            back_im = jnp.zeros((1, rhs_count), jnp.float32)
        square_all, cross_re, cross_im, coef_re, coef_im, back_re, back_im = (
            by_axis(square_loc, TA),
            by_axis(cross_re, TA),
            by_axis(cross_im, TA),
            by_axis(coef_re, TA),
            by_axis(coef_im, TA),
            by_axis(back_re, TA),
            by_axis(back_im, TA),
        )
        squared = square_all
        proj_re = cross_re
        proj_im = cross_im
        for number in range(iteration):
            mapped = mapped - scaled(basis_q[number], coef_re[number], coef_im[number], comp_count)
            direction = direction - scaled(
                basis_p[number], coef_re[number], coef_im[number], comp_count
            )
            squared = squared - (
                coef_re[number] * coef_re[number] + coef_im[number] * coef_im[number]
            )
            proj_re = proj_re - (
                coef_re[number] * back_re[number] + coef_im[number] * back_im[number]
            )
            proj_im = proj_im - (
                coef_re[number] * back_im[number] - coef_im[number] * back_re[number]
            )
        factor = 1.0 / jnp.sqrt(squared + 1e-06)
        unit_q = mapped * factor
        unit_p = direction * factor
        alpha_re = proj_re * factor
        alpha_im = proj_im * factor
        solution = solution + scaled(unit_p, alpha_re, alpha_im, comp_count)
        residual = residual - scaled(unit_q, alpha_re, alpha_im, comp_count)
        basis_q.append(unit_q)
        basis_p.append(unit_p)
    return (
        solution.reshape(1, site_count, 2 * comp_count, rhs_count),
        residual.reshape(1, site_count, 2 * comp_count, rhs_count),
    )


def solution(mesh):
    finer = Mesh(mesh.devices.reshape(mesh.shape["cfg"], 8, 8, 2), ("cfg", "ta_0", "ta_1", "ta_2"))
    placed = (
        P("cfg", TA, None, None, None, None),
        P(CFG_TA, None, None),
        P(CFG_TA, None, None, None),
        P("cfg"),
    )
    return jax.shard_map(
        shards,
        mesh=finer,
        in_specs=placed,
        out_specs=(P(CFG_TA, None, None, None), P(CFG_TA, None, None, None)),
        check_vma=False,
    )
```

profile of v0, /device:TPU:517, one launch (start us, length us, event | category | flops | bytes accessed | tf_op | source)
XLA Modules:
  0.0 360.2 jit_solution(12896941570279861688)
XLA Ops:
  0.6 28.2 %all-to-all-start = ((bf16[128,1,2,2,24,128]{5,4,3,2,1,0:T(8,128)(2,1)}), bf16[128,1,2,2,24,128]{5,4,3,2,1,0:T(8,128)(2,1)}, u32[]{:S(2)}, u32[]{:S(2)}) async-start(bf16[128,1,2,2,24,128]{5,4,3,2,1,0:T(8,128)(2,1)} %param.4), calls=%async_computation | async-start | bytes 6291456 | tf_op jit(solution)/shard_map/all_to_all | solution.py:65
  28.9 10.7 %reshape.404 = bf16[8,16,2,24,2,24]{5,4,3,2,1,0:T(2,128)(2,1)S(1)} reshape(bf16[1,128,2304]{2,1,0:T(8,128)(2,1)} %param.5) | data formatting | bytes 1179648 | tf_op jit(solution)/shard_map/reshape | solution.py:68
  39.6 5.7 %fusion.63 = (bf16[8,16,2,24,1,24]{5,4,3,2,1,0:T(2,128)(2,1)}, bf16[8,16,2,24,1,24]{5,4,3,2,1,0:T(2,128)(2,1)S(1)}) fusion(bf16[8,16,2,24,2,24]{5,4,3,2,1,0:T(2,128)(2,1)S(1)} %reshape.404), kind=kLoop, calls=%fused_computation.200 | loop fusion | bytes 1179648 | tf_op jit(solution)/shard_map/slice | solution.py:28
  45.7 3.8 %reshape.402 = bf16[8,48,9,2,48]{4,3,2,1,0:T(2,128)(2,1)S(1)} reshape(bf16[1,8,48,864]{3,2,1,0:T(8,128)(2,1)} %param.6) | data formatting | bytes 1327104 | tf_op jit(solution)/shard_map/reshape | solution.py:74
  49.5 4.4 %slice_negate_fusion = (bf16[8,48,9,1,48]{4,3,2,1,0:T(2,128)(2,1)S(1)}, bf16[8,48,9,1,48]{4,3,2,1,0:T(2,128)(2,1)S(1)}, bf16[8,48,9,1,48]{4,3,2,1,0:T(2,128)(2,1)S(1)}) fusion(bf16[8,48,9,2,48]{4,3,2,1,0:T(2,128)(2,1)S(1)} %reshape.402), kind=kLoop, calls=%fused_computation.196 | loop fusion | flops 165888 | bytes 1658880 | tf_op jit(solution)/shard_map/neg | solution.py:77
  53.9 9.7 %maximum_bitcast_fusion.2 = (bf16[8,1,48,9,2,48]{5,4,3,2,1,0:T(2,128)(2,1)S(1)}, bf16[8,1,48,9,2,48]{5,4,3,2,1,0:T(2,128)(2,1)S(1)}) fusion(bf16[8,48,9,1,48]{4,3,2,1,0:T(2,128)(2,1)S(1)} %get-tuple-element.92, bf16[8,48,9,1,48]{4,3,2,1,0:T(2,128)(2,1)S(1)} %get-tuple-element.94, bf16[8,48,9,1,48]{4,3,2,1,0:T(2,128)(2,1)S(1)} %get-tuple-element.93), kind=kLoop, calls=%fused_computation.8 | loop fusion | flops 2654208 | bytes 2322432 | tf_op jit(solution)/shard_map/stack | solution.py:79
  63.6 7.6 %pad_maximum_fusion = bf16[8,2,48,9,2,48]{5,4,3,2,1,0:T(2,128)(2,1)} fusion(bf16[8,1,48,9,2,48]{5,4,3,2,1,0:T(2,128)(2,1)S(1)} %get-tuple-element.91, bf16[8,1,48,9,2,48]{5,4,3,2,1,0:T(2,128)(2,1)S(1)} %get-tuple-element.90), kind=kLoop, calls=%fused_computation.4 | loop fusion | flops 663552 | bytes 2654208 | tf_op jit(solution)/shard_map/stack | solution.py:79
  71.2 6.1 %reshape.403 = bf16[8,96,864]{2,1,0:T(8,128)(2,1)S(1)} reshape(bf16[8,2,48,9,2,48]{5,4,3,2,1,0:T(2,128)(2,1)} %pad_maximum_fusion) | data formatting | bytes 2654208 | tf_op jit(solution)/shard_map/reshape | solution.py:79
  78.0 2.3 fusion.62
  80.3 3.2 maximum_bitcast_fusion
  83.5 18.5 %all-to-all-done = bf16[128,1,2,2,24,128]{5,4,3,2,1,0:T(8,128)(2,1)} async-done(((bf16[128,1,2,2,24,128]{5,4,3,2,1,0:T(8,128)(2,1)}), bf16[128,1,2,2,24,128]{5,4,3,2,1,0:T(8,128)(2,1)}, u32[]{:S(2)}, u32[]{:S(2)}) %all-to-all-start) | async-done | bytes 3145760 | tf_op jit(solution)/shard_map/all_to_all | solution.py:65
  102.0 7.1 %fusion.5 = f32[8,2,2,24,128]{4,3,1,2,0:T(8,128)S(1)} fusion(bf16[8,16,2,2,24,128,1]{5,4,3,2,1,0,6:T(8,128)(2,1)} %bitcast.9, bf16[8,16,1,2,2,24,24]{6,5,1,3,2,4,0:T(8,128)(2,1)} %get-tuple-element.96, bf16[8,16,1,2,2,24,24]{6,5,1,3,2,4,0:T(8,128)(2,1)} %get-tuple-element.95), kind=kOutput, calls=%fused_computation.12 | convolution fusion | flops 151584768 | bytes 4718592 | tf_op jit(solution)/shard_map/sodchvk,sochkr->sdhvr/dot_general | solution.py:70
  109.3 1.5 collective-permute-start
  110.8 1.2 collective-permute-start.2
  112.2 3.4 collective-permute-done
  115.6 2.3 collective-permute-start.1
  117.9 5.4 %collective-permute-start.3 = (bf16[2,8,96,128]{3,2,1,0:T(8,128)(2,1)S(1)}, bf16[2,8,96,128]{3,2,1,0:T(8,128)(2,1)S(1)}, u32[]{:S(2)}, u32[]{:S(2)}) collective-permute-start(bf16[2,8,96,128]{3,2,1,0:T(8,128)(2,1)S(1)} %get-tuple-element.158), channel_id=1, source_target_pairs={{0,120},{1,121},{2,122},{3,123},{4,124},{5,125},{6,126},{7,127},{8... | collective-permute-start | bytes 1179656 | tf_op jit(solution)/shard_map/ppermute | solution.py:17
  123.4 15.3 %collective-permute-done.1 = bf16[2,8,96,128]{3,2,1,0:T(8,128)(2,1)S(1)} collective-permute-done((bf16[2,8,96,128]{3,2,1,0:T(8,128)(2,1)S(1)}, bf16[2,8,96,128]{3,2,1,0:T(8,128)(2,1)S(1)}, u32[]{:S(2)}, u32[]{:S(2)}) %collective-permute-start.1) | collective-permute-done | bytes 393248 | tf_op jit(solution)/shard_map/ppermute | solution.py:17
  138.8 16.5 %collective-permute-done.3 = bf16[2,8,96,128]{3,2,1,0:T(8,128)(2,1)S(1)} collective-permute-done((bf16[2,8,96,128]{3,2,1,0:T(8,128)(2,1)S(1)}, bf16[2,8,96,128]{3,2,1,0:T(8,128)(2,1)S(1)}, u32[]{:S(2)}, u32[]{:S(2)}) %collective-permute-start.3) | collective-permute-done | bytes 393248 | tf_op jit(solution)/shard_map/ppermute | solution.py:17
  155.5 0.6 convolution_add_fusion.2
  156.2 11.3 %all-reduce.5 = (f32[128]{0:T(128)S(1)}, f32[128]{0:T(128)S(1)}, f32[128]{0:T(128)S(1)}) all-reduce(f32[128]{0:T(128)S(1)} %get-tuple-element.28, f32[128]{0:T(128)S(1)} %get-tuple-element.19, f32[128]{0:T(128)S(1)} %get-tuple-element.18), channel_id=1, replica_groups=mesh['cfg'=2,'ta_0'=8,'ta_1'=8,'ta_2'=2] {'ta_0'}, use_global_device_ids=true, to_apply=%region_5.6 | all-reduce | flops 384 | bytes 3072 | tf_op jit(solution)/shard_map/psum | solution.py:22
  167.5 13.1 %all-reduce.2 = (f32[128]{0:T(128)S(1)}, f32[128]{0:T(128)S(1)}, f32[128]{0:T(128)S(1)}) all-reduce(f32[128]{0:T(128)S(1)} %get-tuple-element.60, f32[128]{0:T(128)S(1)} %get-tuple-element.61, f32[128]{0:T(128)S(1)} %get-tuple-element.62), channel_id=1, replica_groups=mesh['cfg'=2,'ta_0'=8,'ta_1'=8,'ta_2'=2] {'ta_1'}, use_global_device_ids=true, to_apply=%region_6.7 | all-reduce | flops 384 | bytes 3072 | tf_op jit(solution)/shard_map/psum | solution.py:22
  180.5 10.7 %all-reduce.8 = (f32[128]{0:T(128)S(1)}, f32[128]{0:T(128)S(1)}, f32[128]{0:T(128)S(1)}) all-reduce(f32[128]{0:T(128)S(1)} %get-tuple-element.43, f32[128]{0:T(128)S(1)} %get-tuple-element.44, f32[128]{0:T(128)S(1)} %get-tuple-element.45), channel_id=1, replica_groups=mesh['cfg'=2,'ta_0'=8,'ta_1'=8,'ta_2'=2] {'ta_2'}, use_global_device_ids=true, to_apply=%region_7.8 | all-reduce | flops 384 | bytes 3072 | tf_op jit(solution)/shard_map/psum | solution.py:22
  191.3 0.9 fusion.61
  192.5 1.4 collective-permute-start.6
  194.3 3.3 collective-permute-done.4
  197.7 2.2 collective-permute-start.5
  199.9 5.5 %collective-permute-start.7 = (bf16[2,8,96,128]{3,2,1,0:T(8,128)(2,1)S(1)}, bf16[2,8,96,128]{3,2,1,0:T(8,128)(2,1)S(1)}, u32[]{:S(2)}, u32[]{:S(2)}) collective-permute-start(bf16[2,8,96,128]{3,2,1,0:T(8,128)(2,1)S(1)} %get-tuple-element.150), channel_id=1, source_target_pairs={{0,120},{1,121},{2,122},{3,123},{4,124},{5,125},{6,126},{7,127},{8... | collective-permute-start | bytes 1179656 | tf_op jit(solution)/shard_map/ppermute | solution.py:17
  205.5 13.4 %collective-permute-done.5 = bf16[2,8,96,128]{3,2,1,0:T(8,128)(2,1)S(1)} collective-permute-done((bf16[2,8,96,128]{3,2,1,0:T(8,128)(2,1)S(1)}, bf16[2,8,96,128]{3,2,1,0:T(8,128)(2,1)S(1)}, u32[]{:S(2)}, u32[]{:S(2)}) %collective-permute-start.5) | collective-permute-done | bytes 393248 | tf_op jit(solution)/shard_map/ppermute | solution.py:17
  218.9 5.3 %collective-permute-done.7 = bf16[2,8,96,128]{3,2,1,0:T(8,128)(2,1)S(1)} collective-permute-done((bf16[2,8,96,128]{3,2,1,0:T(8,128)(2,1)S(1)}, bf16[2,8,96,128]{3,2,1,0:T(8,128)(2,1)S(1)}, u32[]{:S(2)}, u32[]{:S(2)}) %collective-permute-start.7) | collective-permute-done | bytes 393248 | tf_op jit(solution)/shard_map/ppermute | solution.py:17
  224.5 0.6 convolution_add_fusion.1
  225.3 25.2 %all-reduce.4 = (f32[1,128]{1,0:T(1,128)S(1)}, f32[1,128]{1,0:T(1,128)S(1)}, f32[128]{0:T(128)S(1)}, f32[128]{0:T(128)S(1)}, f32[1,128]{1,0:T(1,128)S(1)}, /*index=5*/f32[1,128]{1,0:T(1,128)S(1)}, f32[128]{0:T(128)S(1)}) all-reduce(f32[1,128]{1,0:T(1,128)S(1)} %bitcast.355, ...), channel_id=1, replica_groups=mesh['cfg'=2,'ta_0'=8,'ta_1'=8,'ta_2'=2] {'ta_0'}, use_global_device_ids=true, to_apply=%region_25.26 | all-reduce | flops 896 | bytes 7168 | tf_op jit(solution)/shard_map/psum | solution.py:22
  250.5 13.2 %all-reduce.1 = (f32[1,128]{1,0:T(1,128)S(1)}, f32[1,128]{1,0:T(1,128)S(1)}, f32[128]{0:T(128)S(1)}, f32[128]{0:T(128)S(1)}, f32[1,128]{1,0:T(1,128)S(1)}, /*index=5*/f32[1,128]{1,0:T(1,128)S(1)}, f32[128]{0:T(128)S(1)}) all-reduce(f32[1,128]{1,0:T(1,128)S(1)} %get-tuple-element.53, ...), channel_id=1, replica_groups=mesh['cfg'=2,'ta_0'=8,'ta_1'=8,'ta_2'=2] {'ta_1'}, use_global_device_ids=true, to_apply=%region_26.27 | all-reduce | flops 896 | bytes 7168 | tf_op jit(solution)/shard_map/psum | solution.py:22
  263.7 9.8 %all-reduce.7 = (f32[128]{0:T(128)S(1)}, f32[128]{0:T(128)S(1)}, f32[128]{0:T(128)S(1)}, f32[128]{0:T(128)S(1)}, f32[128]{0:T(128)S(1)}, /*index=5*/f32[128]{0:T(128)S(1)}, f32[128]{0:T(128)S(1)}) all-reduce(f32[128]{0:T(128)S(1)} %bitcast.364, f32[128]{0:T(128)S(1)} %bitcast.365, ...), channel_id=1, replica_groups=mesh['cfg'=2,'ta_0'=8,'ta_1'=8,'ta_2'=2] {'ta_2'}, use_global_device_ids=true, to_apply=%region_27.28 | all-reduce | flops 896 | bytes 7168 | tf_op jit(solution)/shard_map/psum | solution.py:22
  273.8 0.5 collective-permute-start.8
  274.3 1.6 collective-permute-start.10
  276.2 3.1 collective-permute-done.8
  279.4 2.2 collective-permute-start.9
  281.7 5.5 %collective-permute-start.11 = (bf16[2,8,96,128]{3,2,1,0:T(8,128)(2,1)S(1)}, bf16[2,8,96,128]{3,2,1,0:T(8,128)(2,1)S(1)}, u32[]{:S(2)}, u32[]{:S(2)}) collective-permute-start(bf16[2,8,96,128]{3,2,1,0:T(8,128)(2,1)S(1)} %get-tuple-element.142), channel_id=1, source_target_pairs={{0,120},{1,121},{2,122},{3,123},{4,124},{5,125},{6,126},{7,127},{8... | collective-permute-start | bytes 1179656 | tf_op jit(solution)/shard_map/ppermute | solution.py:17
  287.2 18.1 %collective-permute-done.9 = bf16[2,8,96,128]{3,2,1,0:T(8,128)(2,1)S(1)} collective-permute-done((bf16[2,8,96,128]{3,2,1,0:T(8,128)(2,1)S(1)}, bf16[2,8,96,128]{3,2,1,0:T(8,128)(2,1)S(1)}, u32[]{:S(2)}, u32[]{:S(2)}) %collective-permute-start.9) | collective-permute-done | bytes 393248 | tf_op jit(solution)/shard_map/ppermute | solution.py:17
  305.7 0.6 convolution_add_fusion
  306.7 0.4 copy-done.4
  307.1 26.2 %all-reduce.3 = (f32[2,128]{1,0:T(2,128)S(1)}, f32[2,128]{1,0:T(2,128)S(1)}, f32[128]{0:T(128)S(1)}, f32[128]{0:T(128)S(1)}, f32[2,128]{1,0:T(2,128)S(1)}, /*index=5*/f32[2,128]{1,0:T(2,128)S(1)}, f32[128]{0:T(128)S(1)}) all-reduce(f32[2,128]{1,0:T(2,128)S(1)} %pad_maximum_fusion.18, ...), channel_id=1, replica_groups=mesh['cfg'=2,'ta_0'=8,'ta_1'=8,'ta_2'=2] {'ta_0'}, use_global_device_ids=true, to_apply=%region_56.57 | all-reduce | flops 1408 | bytes 11264 | tf_op jit(solution)/shard_map/psum | solution.py:22
  333.3 13.4 %all-reduce = (f32[2,128]{1,0:T(2,128)S(1)}, f32[2,128]{1,0:T(2,128)S(1)}, f32[128]{0:T(128)S(1)}, f32[128]{0:T(128)S(1)}, f32[2,128]{1,0:T(2,128)S(1)}, /*index=5*/f32[2,128]{1,0:T(2,128)S(1)}, f32[128]{0:T(128)S(1)}) all-reduce(f32[2,128]{1,0:T(2,128)S(1)} %get-tuple-element.46, ...), channel_id=1, replica_groups=mesh['cfg'=2,'ta_0'=8,'ta_1'=8,'ta_2'=2] {'ta_1'}, use_global_device_ids=true, to_apply=%region_57.58 | all-reduce | flops 1408 | bytes 11264 | tf_op jit(solution)/shard_map/psum | solution.py:22
  346.8 9.9 %all-reduce.6 = (f32[2,128]{1,0:T(2,128)S(1)}, f32[2,128]{1,0:T(2,128)S(1)}, f32[128]{0:T(128)S(1)}, f32[128]{0:T(128)S(1)}, f32[2,128]{1,0:T(2,128)S(1)}, /*index=5*/f32[2,128]{1,0:T(2,128)S(1)}, f32[128]{0:T(128)S(1)}) all-reduce(f32[2,128]{1,0:T(2,128)S(1)} %get-tuple-element.29, ...), channel_id=1, replica_groups=mesh['cfg'=2,'ta_0'=8,'ta_1'=8,'ta_2'=2] {'ta_2'}, use_global_device_ids=true, to_apply=%region_58.59 | all-reduce | flops 1408 | bytes 11264 | tf_op jit(solution)/shard_map/psum | solution.py:22
  357.0 0.7 copy-done.1
  358.3 0.8 maximum_subtract_fusion.12
  359.2 0.8 fusion.10
  (101 shorter events, 4.8 us)
Async XLA Ops:
  0.6 101.4 %all-to-all-start = ((bf16[128,1,2,2,24,128]{5,4,3,2,1,0:T(8,128)(2,1)}), bf16[128,1,2,2,24,128]{5,4,3,2,1,0:T(8,128)(2,1)}, u32[]{:S(2)}, u32[]{:S(2)}) async-start(bf16[128,1,2,2,24,128]{5,4,3,2,1,0:T(8,128)(2,1)} %param.4), calls=%async_computation | async-start | bytes 6291456 | tf_op jit(solution)/shard_map/all_to_all | solution.py:65
  109.3 6.2 %collective-permute-start = (bf16[8,96,128]{2,1,0:T(8,128)(2,1)S(1)}, bf16[8,96,128]{2,1,0:T(8,128)(2,1)S(1)}, u32[]{:S(2)}, u32[]{:S(2)}) collective-permute-start(bf16[8,96,128]{2,1,0:T(8,128)(2,1)S(1)} %bitcast_convert_fusion), channel_id=1, source_target_pairs={{0,127},{1,0},{2,1},{3,2},{4,3},{5,4},{6,5},{7,6},{8,7},{9,8},{10,... | collective-permute-start | bytes 589832 | tf_op jit(solution)/shard_map/ppermute | solution.py:17
  110.8 4.7 %collective-permute-start.2 = (bf16[8,96,128]{2,1,0:T(8,128)(2,1)S(1)}, bf16[8,96,128]{2,1,0:T(8,128)(2,1)S(1)}, u32[]{:S(2)}, u32[]{:S(2)}) collective-permute-start(bf16[8,96,128]{2,1,0:T(8,128)(2,1)S(1)} %bitcast_convert_fusion), channel_id=1, source_target_pairs={{0,1},{1,2},{2,3},{3,4},{4,5},{5,6},{6,7},{7,8},{8,9},{9,10},{10,1... | collective-permute-start | bytes 589832 | tf_op jit(solution)/shard_map/ppermute | solution.py:17
  115.6 23.1 %collective-permute-start.1 = (bf16[2,8,96,128]{3,2,1,0:T(8,128)(2,1)S(1)}, bf16[2,8,96,128]{3,2,1,0:T(8,128)(2,1)S(1)}, u32[]{:S(2)}, u32[]{:S(2)}) collective-permute-start(bf16[2,8,96,128]{3,2,1,0:T(8,128)(2,1)S(1)} %get-tuple-element.159), channel_id=1, source_target_pairs={{0,8},{1,9},{2,10},{3,11},{4,12},{5,13},{6,14},{7,15},{8,16},{9,17... | collective-permute-start | bytes 1179656 | tf_op jit(solution)/shard_map/ppermute | solution.py:17
  117.9 37.3 %collective-permute-start.3 = (bf16[2,8,96,128]{3,2,1,0:T(8,128)(2,1)S(1)}, bf16[2,8,96,128]{3,2,1,0:T(8,128)(2,1)S(1)}, u32[]{:S(2)}, u32[]{:S(2)}) collective-permute-start(bf16[2,8,96,128]{3,2,1,0:T(8,128)(2,1)S(1)} %get-tuple-element.158), channel_id=1, source_target_pairs={{0,120},{1,121},{2,122},{3,123},{4,124},{5,125},{6,126},{7,127},{8... | collective-permute-start | bytes 1179656 | tf_op jit(solution)/shard_map/ppermute | solution.py:17
  192.2 5.4 %collective-permute-start.4 = (bf16[8,96,128]{2,1,0:T(8,128)(2,1)S(1)}, bf16[8,96,128]{2,1,0:T(8,128)(2,1)S(1)}, u32[]{:S(2)}, u32[]{:S(2)}) collective-permute-start(bf16[8,96,128]{2,1,0:T(8,128)(2,1)S(1)} %get-tuple-element.84), channel_id=1, source_target_pairs={{0,127},{1,0},{2,1},{3,2},{4,3},{5,4},{6,5},{7,6},{8,7},{9,8},{10,... | collective-permute-start | bytes 589832 | tf_op jit(solution)/shard_map/ppermute | solution.py:17
  192.5 5.0 %collective-permute-start.6 = (bf16[8,96,128]{2,1,0:T(8,128)(2,1)S(1)}, bf16[8,96,128]{2,1,0:T(8,128)(2,1)S(1)}, u32[]{:S(2)}, u32[]{:S(2)}) collective-permute-start(bf16[8,96,128]{2,1,0:T(8,128)(2,1)S(1)} %get-tuple-element.84), channel_id=1, source_target_pairs={{0,1},{1,2},{2,3},{3,4},{4,5},{5,6},{6,7},{7,8},{8,9},{9,10},{10,1... | collective-permute-start | bytes 589832 | tf_op jit(solution)/shard_map/ppermute | solution.py:17
  197.7 21.2 %collective-permute-start.5 = (bf16[2,8,96,128]{3,2,1,0:T(8,128)(2,1)S(1)}, bf16[2,8,96,128]{3,2,1,0:T(8,128)(2,1)S(1)}, u32[]{:S(2)}, u32[]{:S(2)}) collective-permute-start(bf16[2,8,96,128]{3,2,1,0:T(8,128)(2,1)S(1)} %get-tuple-element.151), channel_id=1, source_target_pairs={{0,8},{1,9},{2,10},{3,11},{4,12},{5,13},{6,14},{7,15},{8,16},{9,17... | collective-permute-start | bytes 1179656 | tf_op jit(solution)/shard_map/ppermute | solution.py:17
  199.9 24.4 %collective-permute-start.7 = (bf16[2,8,96,128]{3,2,1,0:T(8,128)(2,1)S(1)}, bf16[2,8,96,128]{3,2,1,0:T(8,128)(2,1)S(1)}, u32[]{:S(2)}, u32[]{:S(2)}) collective-permute-start(bf16[2,8,96,128]{3,2,1,0:T(8,128)(2,1)S(1)} %get-tuple-element.150), channel_id=1, source_target_pairs={{0,120},{1,121},{2,122},{3,123},{4,124},{5,125},{6,126},{7,127},{8... | collective-permute-start | bytes 1179656 | tf_op jit(solution)/shard_map/ppermute | solution.py:17
  273.7 32.7 %copy-start = (f32[8,96,128]{2,1,0:T(8,128)}, f32[8,96,128]{2,1,0:T(8,128)S(1)}, u32[]{:S(2)}) copy-start(f32[8,96,128]{2,1,0:T(8,128)S(1)} %fusion.12) | copy-start | bytes 1179652
  273.8 32.5 %copy-start.2 = (f32[8,96,128]{2,1,0:T(8,128)}, f32[8,96,128]{2,1,0:T(8,128)S(1)}, u32[]{:S(2)}) copy-start(f32[8,96,128]{2,1,0:T(8,128)S(1)} %get-tuple-element.83) | copy-start | bytes 1179652
  273.8 5.5 %collective-permute-start.8 = (bf16[8,96,128]{2,1,0:T(8,128)(2,1)S(1)}, bf16[8,96,128]{2,1,0:T(8,128)(2,1)S(1)}, u32[]{:S(2)}, u32[]{:S(2)}) collective-permute-start(bf16[8,96,128]{2,1,0:T(8,128)(2,1)S(1)} %get-tuple-element.82), channel_id=1, source_target_pairs={{0,127},{1,0},{2,1},{3,2},{4,3},{5,4},{6,5},{7,6},{8,7},{9,8},{10,... | collective-permute-start | bytes 589832 | tf_op jit(solution)/shard_map/ppermute | solution.py:17
  274.3 5.0 %collective-permute-start.10 = (bf16[8,96,128]{2,1,0:T(8,128)(2,1)S(1)}, bf16[8,96,128]{2,1,0:T(8,128)(2,1)S(1)}, u32[]{:S(2)}, u32[]{:S(2)}) collective-permute-start(bf16[8,96,128]{2,1,0:T(8,128)(2,1)S(1)} %get-tuple-element.82), channel_id=1, source_target_pairs={{0,1},{1,2},{2,3},{3,4},{4,5},{5,6},{6,7},{7,8},{8,9},{9,10},{10,1... | collective-permute-start | bytes 589832 | tf_op jit(solution)/shard_map/ppermute | solution.py:17
  279.4 26.0 %collective-permute-start.9 = (bf16[2,8,96,128]{3,2,1,0:T(8,128)(2,1)S(1)}, bf16[2,8,96,128]{3,2,1,0:T(8,128)(2,1)S(1)}, u32[]{:S(2)}, u32[]{:S(2)}) collective-permute-start(bf16[2,8,96,128]{3,2,1,0:T(8,128)(2,1)S(1)} %get-tuple-element.143), channel_id=1, source_target_pairs={{0,8},{1,9},{2,10},{3,11},{4,12},{5,13},{6,14},{7,15},{8,16},{9,17... | collective-permute-start | bytes 1179656 | tf_op jit(solution)/shard_map/ppermute | solution.py:17
  281.7 23.8 %collective-permute-start.11 = (bf16[2,8,96,128]{3,2,1,0:T(8,128)(2,1)S(1)}, bf16[2,8,96,128]{3,2,1,0:T(8,128)(2,1)S(1)}, u32[]{:S(2)}, u32[]{:S(2)}) collective-permute-start(bf16[2,8,96,128]{3,2,1,0:T(8,128)(2,1)S(1)} %get-tuple-element.142), channel_id=1, source_target_pairs={{0,120},{1,121},{2,122},{3,123},{4,124},{5,125},{6,126},{7,127},{8... | collective-permute-start | bytes 1179656 | tf_op jit(solution)/shard_map/ppermute | solution.py:17
  306.3 0.7 copy-start.4
  306.3 50.4 %copy-start.6 = (f32[8,96,128]{2,1,0:T(8,128)S(1)}, f32[8,96,128]{2,1,0:T(8,128)}, u32[]{:S(2)}) copy-start(f32[8,96,128]{2,1,0:T(8,128)} %get-tuple-element.141) | copy-start | bytes 1179652
  356.7 1.0 copy-start.1
  356.9 1.0 copy-start.3
  356.9 1.1 copy-start.5
where the time goes:
time: 367 us; the launch traced here: 360 us
  blocking collectives  133 us (36%)
  waiting for transfers between devices  96.9 us (26%)
  starting transfers between devices  57.8 us (16%)
  other arithmetic  32.5 us (9%)
  local copies, waits for them, and re-layouts  29.1 us (8%)
  matrix products  8.85 us (2%)
    psum x9, blocking collectives, by_axis(): array = lax.psum(array, axis)  133 us
    ppermute x12, waiting for transfers between devices, from_behind(): return lax.ppermute(value, axis, pairs)  78.4 us
    ppermute x12, starting transfers between devices, from_behind(): return lax.ppermute(value, axis, pairs)  29.6 us
    all_to_all x1, starting transfers between devices, shards(): lax.all_to_all(fine_source, TA, split_axis=0, concat_axis=1, tiled=True)  28.2 us
    all_to_all x1, waiting for transfers between devices, shards(): lax.all_to_all(fine_source, TA, split_axis=0, concat_axis=1, tiled=True)  18.5 us
    another operation x2, other arithmetic, shards(): jnp.stack([upper_rows, lower_rows], axis=1)  17.3 us
    reshape x1, local copies, waits for them, and re-layouts, shards(): projectors.reshape(site_count, block_count, 2, null_count, 2, fine_count)  10.7 us
  transfers between devices with their start and end apart: 13, of which 9 were waited for; matrix products, arithmetic and copies ran while one was open for 15% of the time, Pallas kernels for 0%

commit v1 on v0

v1 whole, which is shorter than its diff:
```python
import functools

import jax
import jax.numpy as jnp
from jax import lax
from jax.experimental import pallas as pl
from jax.experimental.pallas import tpu as pltpu
from jax.sharding import Mesh
from jax.sharding import PartitionSpec as P

YC, XC, CORES = 8, 8, 2
LX = 4
HALF = XC // 2
ITERS = 3
GROUP = ("y", "x", "core")
ALL = ("cfg", "y", "x", "core")
MESH = pl.DeviceIdType.MESH
CHUNKS = 2
F32, BF16 = jnp.float32, jnp.bfloat16


def slot_of(x, core):
    z = 2 * (x % HALF) + core
    return (XC - z) % XC, 1 - x // HALF


def home_of(x, core):
    z = (XC - x) % XC
    return HALF * (1 - core) + z // 2, z % 2


def real_weights(proj_view):
    proj_re = proj_view[..., 0, :]
    proj_im = proj_view[..., 1, :]
    first_row = jnp.stack([proj_re, proj_im], axis=-4)
    second_row = jnp.stack([-proj_im, proj_re], axis=-4)
    return jnp.stack([first_row, second_row], axis=-5)


def solve_kernel(
    mass_ref, source_ref, links_ref, sol_ref, res_ref,
    r_buf, w_buf, halo, q_buf, p_buf, row_send, row_recv, col_send, col_recv, out_send, out_recv,
    src_ss, src_rs, halo_ss, halo_rs, row_ss, row_rs, col_ss, col_rs, out_ss, out_rs,
):
    sites, full, rhs = source_ref.shape
    comps = full // 2
    part = sites // CHUNKS
    g, y, x, core = (lax.axis_index(name) for name in ALL)
    rem, div = lax.rem, lax.div
    z_home = 2 * rem(x, HALF) + core
    to_slot = (g, y, rem(XC - z_home, XC), 1 - div(x, HALF))
    z_slot = rem(XC - x, XC)
    to_home = (g, y, HALF * (1 - core) + div(z_slot, 2), rem(z_slot, 2))
    odd = 1 - core
    upper = (g, y, rem(x + XC - 1, XC), core)
    lower = (g, y, rem(x + 1, XC), core)
    mate = (g, y, x, 1 - core)
    beyond = (g, rem(y + YC - 1 + 2 * odd, YC), x, 1 - core)
    row_peers = [
        (g, y, rem(x + d // 2, XC), rem(core + d % 2, CORES)) for d in range(1, XC * CORES)
    ]
    col_peers = [(g, rem(y + d, YC), x, core) for d in range(1, YC)]

    barrier = pltpu.get_barrier_semaphore()
    everyone = row_peers + col_peers + [beyond]
    for peer in everyone:
        pl.semaphore_signal(barrier, inc=1, device_id=peer, device_id_type=MESH)
    pl.semaphore_wait(barrier, len(everyone))

    def remote(src, dst, send_sem, recv_sem, peer):
        return pltpu.make_async_remote_copy(
            src_ref=src, dst_ref=dst, send_sem=send_sem, recv_sem=recv_sem,
            device_id=peer, device_id_type=MESH,
        )

    def chunk(c):
        return pl.ds(c * part, part)

    pending = []

    def start(copy):
        copy.start()
        pending.append(copy)

    for c in range(CHUNKS):
        start(remote(source_ref.at[chunk(c)], r_buf.at[0, chunk(c)], src_ss.at[c], src_rs.at[c], to_slot))

    def send_halo(k, c):
        src = w_buf.at[k, chunk(c)]
        for kind, peer in ((1, upper), (0, lower), (3 - odd, mate), (2 + odd, beyond)):
            place = {0: 0, 1: 1}.get(kind, 2) if isinstance(kind, int) else (2 if peer is mate else 3)
            start(
                remote(
                    src, halo.at[k, kind, chunk(c)], halo_ss.at[k, place, c], halo_rs.at[k, kind, c], peer
                )
            )

    def wait_halo(k):
        for kind in range(4):
            for c in range(CHUNKS):
                remote(
                    w_buf.at[k, chunk(c)], halo.at[k, kind, chunk(c)],
                    halo_ss.at[k, 0, c], halo_rs.at[k, kind, c], mate,
                ).wait_recv()

    def split(array):
        return array[:comps], array[comps:]

    def gains(vectors):
        rows = []
        for vector in vectors:
            re, im = split(vector)
            rows.append(
                jnp.concatenate(
                    [jnp.concatenate([re, im], axis=1), jnp.concatenate([-im, re], axis=1)], axis=0
                )
            )
        return jnp.concatenate(rows, axis=0)

    def folded(array):
        return jnp.sum(array.reshape(comps // 8, 8, rhs), axis=0)

    mass = mass_ref[0]
    span = 4 * full

    def matvec(k):
        local = []
        for s in range(sites):
            line, col = s // LX, s % LX
            near = [
                s,
                line * LX + (col + 1) % LX,
                line * LX + (col + LX - 1) % LX,
                (s + LX) % sites,
            ]
            local.append(
                jnp.dot(
                    links_ref[s, :, 0:span], gains([w_buf[k, n] for n in near]),
                    preferred_element_type=F32,
                )
            )
        wait_halo(k)
        sums = None
        for s in range(sites):
            second = gains(
                [w_buf[k, (s + sites - LX) % sites]] + [halo[k, kind, s] for kind in range(3)]
            )
            third = gains([halo[k, 3, s]])
            out = local[s]
            out = out + jnp.dot(links_ref[s, :, span:2 * span], second, preferred_element_type=F32)
            out = out + jnp.dot(links_ref[s, :, 2 * span:], third, preferred_element_type=F32)
            own_re, own_im = split(w_buf[k, s].astype(F32))
            q_re = out[:, :rhs] + mass * own_re
            q_im = out[:, rhs:] + mass * own_im
            q_buf[k, s, 0:comps] = q_re
            q_buf[k, s, comps:full] = q_im
            r_re, r_im = split(r_buf[k, s])
            terms = [
                folded(q_re * q_re + q_im * q_im),
                folded(q_re * r_re + q_im * r_im),
                folded(q_re * r_im - q_im * r_re),
            ]
            for j in range(k):
                e_re, e_im = split(q_buf[j, s])
                terms += [
                    folded(e_re * q_re + e_im * q_im),
                    folded(e_re * q_im - e_im * q_re),
                    folded(e_re * r_re + e_im * r_im),
                    folded(e_re * r_im - e_im * r_re),
                ]
            sums = terms if sums is None else [a + b for a, b in zip(sums, terms)]
        return [jnp.sum(one, axis=0, keepdims=True) for one in sums]

    def all_reduce(k, sums):
        count = len(sums)
        rows = pl.ds(0, count)
        for i, one in enumerate(sums):
            row_send[k, i:i + 1, :] = one
        for d, peer in enumerate(row_peers):
            start(
                remote(row_send.at[k, rows], row_recv.at[k, d, rows], row_ss.at[k, d], row_rs.at[k, d], peer)
            )
        total = row_send[k, 0:count]
        for d in range(len(row_peers)):
            remote(
                row_send.at[k, rows], row_recv.at[k, d, rows], row_ss.at[k, d], row_rs.at[k, d], mate
            ).wait_recv()
            total = total + row_recv[k, d, 0:count]
        col_send[k, 0:count] = total
        for d, peer in enumerate(col_peers):
            start(
                remote(col_send.at[k, rows], col_recv.at[k, d, rows], col_ss.at[k, d], col_rs.at[k, d], peer)
            )
        for d in range(len(col_peers)):
            remote(
                col_send.at[k, rows], col_recv.at[k, d, rows], col_ss.at[k, d], col_rs.at[k, d], mate
            ).wait_recv()
            total = total + col_recv[k, d, 0:count]
        return [total[i:i + 1] for i in range(count)]

    def minus(value, coefs, basis, s):
        re, im = split(value)
        for j, (c_re, c_im) in enumerate(coefs):
            e_re, e_im = split(basis[j, s])
            re = re - (c_re * e_re - c_im * e_im)
            im = im - (c_re * e_im + c_im * e_re)
        return re, im

    for c in range(CHUNKS):
        remote(source_ref.at[chunk(c)], r_buf.at[0, chunk(c)], src_ss.at[c], src_rs.at[c], mate).wait_recv()
        for s in range(c * part, (c + 1) * part):
            w_buf[0, s] = r_buf[0, s].astype(BF16)
        send_halo(0, c)

    gram = {}
    alphas = []
    factors = []
    for k in range(ITERS):
        totals = all_reduce(k, matvec(k))
        squared, a_re, a_im = totals[:3]
        coefs = []
        for j in range(k):
            c_re, c_im, b_re, b_im = totals[3 + 4 * j:7 + 4 * j]
            coefs.append((c_re, c_im))
            a_re = a_re - (c_re * b_re + c_im * b_im)
            a_im = a_im - (c_re * b_im - c_im * b_re)
        for j, (c_re, c_im) in enumerate(coefs):
            squared = squared - (2.0 - gram[j, j][0]) * (c_re * c_re + c_im * c_im)
        for i in range(k):
            for j in range(i + 1, k):
                (u_re, u_im), (v_re, v_im) = coefs[i], coefs[j]
                m_re = u_re * v_re + u_im * v_im
                m_im = u_re * v_im - u_im * v_re
                n_re, n_im = gram[i, j]
                squared = squared + 2.0 * (m_re * n_re - m_im * n_im)
        squared = jnp.maximum(squared, 0.0)
        factor = 1.0 / jnp.sqrt(squared + 1e-06)
        if k + 1 < ITERS:
            gram[k, k] = (squared * factor * factor, None)
            for j, (c_re, c_im) in enumerate(coefs):
                lack_re = (1.0 - gram[j, j][0]) * c_re
                lack_im = (1.0 - gram[j, j][0]) * c_im
                gram[j, k] = (factor * lack_re, factor * lack_im)
        a_re, a_im = a_re * factor, a_im * factor
        alphas.append((a_re, a_im))
        factors.append(factor)
        last = k + 1 == ITERS
        for c in range(CHUNKS):
            for s in range(c * part, (c + 1) * part):
                q_re, q_im = minus(q_buf[k, s], coefs, q_buf, s)
                q_re, q_im = q_re * factor, q_im * factor
                r_re, r_im = split(r_buf[k, s])
                r_re = r_re - (a_re * q_re - a_im * q_im)
                r_im = r_im - (a_re * q_im + a_im * q_re)
                if last:
                    out_send[1, s, 0:comps] = r_re.astype(BF16)
                    out_send[1, s, comps:full] = r_im.astype(BF16)
                else:
                    q_buf[k, s, 0:comps] = q_re
                    q_buf[k, s, comps:full] = q_im
                    r_buf[k + 1, s, 0:comps] = r_re
                    r_buf[k + 1, s, comps:full] = r_im
                    w_buf[k + 1, s, 0:comps] = r_re.astype(BF16)
                    w_buf[k + 1, s, comps:full] = r_im.astype(BF16)
            if last:
                start(
                    remote(
                        out_send.at[1, chunk(c)], out_recv.at[1, chunk(c)], out_ss.at[1, c], out_rs.at[1, c],
                        to_home,
                    )
                )
            else:
                send_halo(k + 1, c)
        for c in range(CHUNKS):
            for s in range(c * part, (c + 1) * part):
                p_re, p_im = minus(r_buf[k, s], coefs, p_buf, s)
                p_re, p_im = p_re * factor, p_im * factor
                if last:
                    s_re = a_re * p_re - a_im * p_im
                    s_im = a_re * p_im + a_im * p_re
                    for j in range(k):
                        e_re, e_im = split(p_buf[j, s])
                        b_re, b_im = alphas[j]
                        s_re = s_re + (b_re * e_re - b_im * e_im)
                        s_im = s_im + (b_re * e_im + b_im * e_re)
                    out_send[0, s, 0:comps] = s_re.astype(BF16)
                    out_send[0, s, comps:full] = s_im.astype(BF16)
                else:
                    p_buf[k, s, 0:comps] = p_re
                    p_buf[k, s, comps:full] = p_im
            if last:
                start(
                    remote(
                        out_send.at[0, chunk(c)], out_recv.at[0, chunk(c)], out_ss.at[0, c], out_rs.at[0, c],
                        to_home,
                    )
                )
    for which, target in ((1, res_ref), (0, sol_ref)):
        for c in range(CHUNKS):
            remote(
                out_send.at[which, chunk(c)], out_recv.at[which, chunk(c)],
                out_ss.at[which, c], out_rs.at[which, c], mate,
            ).wait_recv()
            for s in range(c * part, (c + 1) * part):
                target[s] = out_recv[which, s].astype(F32)
    for copy in pending:
        copy.wait_send()


def solve(source, links, mass):
    sites, full, rhs = source.shape
    vector = (sites, full, rhs)
    most = 3 + 4 * (ITERS - 1)
    rows = -(-most // 8) * 8
    peers_x, peers_y = XC * CORES - 1, YC - 1
    dma = pltpu.SemaphoreType.DMA
    vmem = pl.BlockSpec(memory_space=pltpu.VMEM)
    return pl.pallas_call(
        solve_kernel,
        out_shape=(jax.ShapeDtypeStruct(vector, F32), jax.ShapeDtypeStruct(vector, F32)),
        in_specs=[pl.BlockSpec(memory_space=pltpu.SMEM), vmem, vmem],
        out_specs=(vmem, vmem),
        scratch_shapes=[
            pltpu.VMEM((ITERS,) + vector, F32),
            pltpu.VMEM((ITERS,) + vector, BF16),
            pltpu.VMEM((ITERS, 4) + vector, BF16),
            pltpu.VMEM((ITERS,) + vector, F32),
            pltpu.VMEM((ITERS - 1,) + vector, F32),
            pltpu.VMEM((ITERS, rows, rhs), F32),
            pltpu.VMEM((ITERS, peers_x, rows, rhs), F32),
            pltpu.VMEM((ITERS, rows, rhs), F32),
            pltpu.VMEM((ITERS, peers_y, rows, rhs), F32),
            pltpu.VMEM((2,) + vector, BF16),
            pltpu.VMEM((2,) + vector, BF16),
            dma((CHUNKS,)), dma((CHUNKS,)),
            dma((ITERS, 4, CHUNKS)), dma((ITERS, 4, CHUNKS)),
            dma((ITERS, peers_x)), dma((ITERS, peers_x)),
            dma((ITERS, peers_y)), dma((ITERS, peers_y)),
            dma((2, CHUNKS)), dma((2, CHUNKS)),
        ],
        compiler_params=pltpu.CompilerParams(
            collective_id=0, has_side_effects=True, vmem_limit_bytes=48 * 1024 * 1024
        ),
        name="gcr_solve",
    )(mass, source, links)


def shards(fine_source, projectors, stencil_links, quark_mass):
    comp_count = stencil_links.shape[2]
    null_count = comp_count // 2
    site_count = stencil_links.shape[1]
    column_count = projectors.shape[1]
    block_count = column_count // site_count
    fine_count = fine_source.shape[4]
    rhs_count = fine_source.shape[5]
    moves = [
        (x * CORES + c, slot_of(x, c)[0] * CORES + slot_of(x, c)[1])
        for x in range(XC) for c in range(CORES)
    ]
    links = lax.ppermute(stencil_links[0], ("x", "core"), moves)
    regrouped = lax.all_to_all(fine_source, GROUP, split_axis=0, concat_axis=1, tiled=True)
    fine_local = regrouped.reshape(site_count, block_count, 2, 2, fine_count, rhs_count)
    weights = real_weights(
        projectors.reshape(site_count, block_count, 2, null_count, 2, fine_count)
    )
    source = jnp.einsum(
        "sodchvk,sochkr->sdhvr", weights, fine_local, preferred_element_type=jnp.float32
    )
    source = source.reshape(site_count, 2 * comp_count, rhs_count)
    solution, residual = solve(source, links, quark_mass)
    return solution[None], residual[None]


def solution(mesh):
    finer = Mesh(mesh.devices.reshape(mesh.shape["cfg"], YC, XC, CORES), ALL)
    placed = (
        P("cfg", GROUP, None, None, None, None),
        P(ALL, None, None),
        P(ALL, None, None, None),
        P("cfg"),
    )
    return jax.shard_map(
        shards,
        mesh=finer,
        in_specs=placed,
        out_specs=(P(ALL, None, None, None), P(ALL, None, None, None)),
        check_vma=False,
    )
```

time: 367 us -> 206 us (0.56); the launches traced: 360 us -> 205 us
  blocking collectives: 133 us -> 0 us
  Pallas kernels: 0 us -> 93.6 us
  waiting for transfers between devices: 96.9 us -> 54.8 us
  other arithmetic: 32.5 us -> 3.65 us
  starting transfers between devices: 57.8 us -> 29.1 us
  local copies, waits for them, and re-layouts: 29.1 us -> 15.7 us
    psum x9 -> x0, blocking collectives: 133 us -> none  [by_axis(): array = lax.psum(array, axis)]
    pallas_call x0 -> x1, Pallas kernels: none -> 93.6 us  [solve(): pl.pallas_call(solve_kernel, out_shape=(jax.ShapeDtypeStruct(vector, F32)...]
    ppermute x12 -> x1, waiting for transfers between devices: 78.4 us -> 0.96 us  [shards(): links = lax.ppermute(stencil_links[0], ('x', 'core'), moves)]
    all_to_all x1, waiting for transfers between devices: 18.5 us -> 53.8 us  [shards(): lax.all_to_all(fine_source, GROUP, split_axis=0, concat_axis=1, tiled=True)]
    ppermute x12 -> x1, starting transfers between devices: 29.6 us -> 1.34 us  [shards(): links = lax.ppermute(stencil_links[0], ('x', 'core'), moves)]
    another operation x9 -> x0, other arithmetic: 17.5 us -> none  [the longest x2 17.3 us: shards(): jnp.stack([upper_rows, lower_rows], axis=1)]
    reshape x2 -> x0, local copies, waits for them, and re-layouts: 9.95 us -> none  [the longest x1 6.15 us: shards(): jnp.stack([upper_rows, lower_rows], axis=1)]
    reshape x1, local copies, waits for them, and re-layouts: 10.7 us -> 6.21 us  [shards(): projectors.reshape(site_count, block_count, 2, null_count, 2, fine_count)]
  transfers between devices with their start and end apart: 13 -> 2, of which waited for: 9 -> 2; matrix products, arithmetic and copies ran while one was open for 15% -> 12% of each run, Pallas kernels for 0% -> 0%
where the time goes in v1:
time: 206 us; the launch traced here: 205 us
  Pallas kernels  93.6 us (45%)
  waiting for transfers between devices  54.8 us (27%)
  starting transfers between devices  29.1 us (14%)
  local copies, waits for them, and re-layouts  15.7 us (8%)
  matrix products  7.1 us (3%)
  other arithmetic  3.65 us (2%)
    pallas_call x1, Pallas kernels, solve(): pl.pallas_call(solve_kernel, out_shape=(jax.ShapeDtypeStruct(vector, F32)...  93.6 us
    all_to_all x1, waiting for transfers between devices, shards(): lax.all_to_all(fine_source, GROUP, split_axis=0, concat_axis=1, tiled=True)  53.8 us
    all_to_all x1, starting transfers between devices, shards(): lax.all_to_all(fine_source, GROUP, split_axis=0, concat_axis=1, tiled=True)  27.7 us
    slice x1, local copies, waits for them, and re-layouts, real_weights(): proj_im = proj_view[..., 1, :]  7.57 us
    dot_general x1, matrix products, shards(): jnp.einsum('sodchvk,sochkr->sdhvr', weights, fine_local, preferred_elemen...  7.1 us
    reshape x1, local copies, waits for them, and re-layouts, shards(): projectors.reshape(site_count, block_count, 2, null_count, 2, fine_count)  6.21 us
  transfers between devices with their start and end apart: 2, of which 2 were waited for; matrix products, arithmetic and copies ran while one was open for 12% of the time, Pallas kernels for 0%

profile of v1, /device:TPU:517, one launch (start us, length us, event | category | flops | bytes accessed | tf_op | source)
XLA Modules:
  0.0 205.2 jit_solution(18274850496133147560)
XLA Ops:
  0.6 0.0 copy-start.1
  0.6 0.0 copy-start
  0.6 27.7 %all-to-all-start = ((bf16[128,1,2,2,24,128]{5,4,3,2,1,0:T(8,128)(2,1)}), bf16[128,1,2,2,24,128]{5,4,3,2,1,0:T(8,128)(2,1)}, u32[]{:S(2)}, u32[]{:S(2)}) async-start(bf16[128,1,2,2,24,128]{5,4,3,2,1,0:T(8,128)(2,1)} %param.4), calls=%async_computation | async-start | bytes 6291456 | tf_op jit(solution)/shard_map/all_to_all | solution.py:361
  28.4 0.0 copy-done.1
  28.4 1.3 collective-permute-start
  29.7 0.0 copy-done
  29.8 6.2 %reshape.27 = bf16[8,16,2,24,2,24]{5,4,3,2,1,0:T(2,128)(2,1)} reshape(bf16[1,128,2304]{2,1,0:T(8,128)(2,1)S(1)} %copy-done) | data formatting | bytes 1179648 | tf_op jit(solution)/shard_map/reshape | solution.py:364
  36.0 7.6 %fusion.12 = (bf16[8,16,2,24,1,24]{5,4,3,2,1,0:T(2,128)(2,1)S(1)}, bf16[8,16,2,24,1,24]{5,4,3,2,1,0:T(2,128)(2,1)S(1)}) fusion(bf16[8,16,2,24,2,24]{5,4,3,2,1,0:T(2,128)(2,1)} %reshape.27), kind=kLoop, calls=%fused_computation.12 | loop fusion | bytes 1179648 | tf_op jit(solution)/shard_map/slice | solution.py:34
  43.5 0.3 copy.32
  44.5 0.4 fusion.11
  45.0 3.2 %maximum_bitcast_fusion = (bf16[8,16,1,2,2,24,24]{6,5,1,3,2,4,0:T(8,128)(2,1)}, bf16[8,16,1,2,2,24,24]{6,5,1,3,2,4,0:T(8,128)(2,1)}) fusion(bf16[8,16,1,2,24,24]{5,4,1,2,3,0:T(8,128)(2,1)S(1)} %get-tuple-element.7, bf16[8,16,1,2,24,24]{5,4,1,2,3,0:T(8,128)(2,1)S(1)} %bitcast.28, bf16[8,16,1,2,24,24]{5,4,1,2,3,0:T(8,128)(2,1)S(1)} %get-tuple-element.6), kind=kLoop, calls=%fused_computation.4 | loop fusion | flops 589824 | bytes 2064384 | tf_op jit(solution)/shard_map/stack | solution.py:37
  48.2 53.8 %all-to-all-done = bf16[128,1,2,2,24,128]{5,4,3,2,1,0:T(8,128)(2,1)} async-done(((bf16[128,1,2,2,24,128]{5,4,3,2,1,0:T(8,128)(2,1)}), bf16[128,1,2,2,24,128]{5,4,3,2,1,0:T(8,128)(2,1)}, u32[]{:S(2)}, u32[]{:S(2)}) %all-to-all-start) | async-done | bytes 3145760 | tf_op jit(solution)/shard_map/all_to_all | solution.py:361
  102.0 7.1 %fusion.5 = f32[8,2,2,24,128]{4,3,1,2,0:T(8,128)S(1)} fusion(bf16[8,16,2,2,24,128,1]{5,4,3,2,1,0,6:T(8,128)(2,1)} %bitcast.6, bf16[8,16,1,2,2,24,24]{6,5,1,3,2,4,0:T(8,128)(2,1)} %get-tuple-element.11, bf16[8,16,1,2,2,24,24]{6,5,1,3,2,4,0:T(8,128)(2,1)} %get-tuple-element.10), kind=kOutput, calls=%fused_computation.9 | convolution fusion | flops 151584768 | bytes 4718592 | tf_op jit(solution)/shard_map/sodchvk,sochkr->sdhvr/dot_general | solution.py:366
  109.2 1.0 collective-permute-done.links_ref
  110.1 93.6 %gcr_solve.1 = (f32[8,96,128]{2,1,0:T(8,128)S(1)}, f32[8,96,128]{2,1,0:T(8,128)S(1)}) custom-call(f32[1]{0:T(128)S(6)} %copy.35.mass_ref, f32[8,96,128]{2,1,0:T(8,128)S(1)} %bitcast.25, bf16[8,48,864]{2,1,0:T(8,128)(2,1)S(1)} %collective-permute-done.links_ref), custom_call_target="tpu_custom_call" | custom-call | tf_op jit(solution)/shard_map/gcr_solve/pallas_call | solution.py:318
  203.7 0.7 copy.36
  204.5 0.7 copy.37
  (1 shorter events, 0.0 us)
Async XLA Ops:
  0.6 27.8 %copy-start.1 = (bf16[1,8,48,864]{3,2,1,0:T(8,128)(2,1)S(1)}, bf16[1,8,48,864]{3,2,1,0:T(8,128)(2,1)}, u32[]{:S(2)}) copy-start(bf16[1,8,48,864]{3,2,1,0:T(8,128)(2,1)} %param.6) | copy-start | bytes 1990660
  0.6 29.1 %copy-start = (bf16[1,128,2304]{2,1,0:T(8,128)(2,1)S(1)}, bf16[1,128,2304]{2,1,0:T(8,128)(2,1)}, u32[]{:S(2)}) copy-start(bf16[1,128,2304]{2,1,0:T(8,128)(2,1)} %param.5) | copy-start | bytes 1769476
  0.6 101.4 %all-to-all-start = ((bf16[128,1,2,2,24,128]{5,4,3,2,1,0:T(8,128)(2,1)}), bf16[128,1,2,2,24,128]{5,4,3,2,1,0:T(8,128)(2,1)}, u32[]{:S(2)}, u32[]{:S(2)}) async-start(bf16[128,1,2,2,24,128]{5,4,3,2,1,0:T(8,128)(2,1)} %param.4), calls=%async_computation | async-start | bytes 6291456 | tf_op jit(solution)/shard_map/all_to_all | solution.py:361
  28.4 81.7 %collective-permute-start = (bf16[8,48,864]{2,1,0:T(8,128)(2,1)S(1)}, bf16[8,48,864]{2,1,0:T(8,128)(2,1)S(1)}, u32[]{:S(2)}, u32[]{:S(2)}) collective-permute-start(bf16[8,48,864]{2,1,0:T(8,128)(2,1)S(1)} %bitcast.29), channel_id=1, source_target_pairs={{0,1},{1,15},{2,13},{3,11},{4,9},{5,7},{6,5},{7,3},{8,0},{9,14},{1... | collective-permute-start | bytes 1990664 | tf_op jit(solution)/shard_map/ppermute | solution.py:360

commit v2 on v1

--- a/solution.py
+++ b/solution.py
@@ -1,5 +1,3 @@
-import functools
-
 import jax
 import jax.numpy as jnp
 from jax import lax
@@ -16,33 +14,19 @@
 ALL = ("cfg", "y", "x", "core")
 MESH = pl.DeviceIdType.MESH
 CHUNKS = 2
+FK = 24
 F32, BF16 = jnp.float32, jnp.bfloat16
 
 
-def slot_of(x, core):
-    z = 2 * (x % HALF) + core
-    return (XC - z) % XC, 1 - x // HALF
-
-
-def home_of(x, core):
-    z = (XC - x) % XC
-    return HALF * (1 - core) + z // 2, z % 2
-
-
-def real_weights(proj_view):
-    proj_re = proj_view[..., 0, :]
-    proj_im = proj_view[..., 1, :]
-    first_row = jnp.stack([proj_re, proj_im], axis=-4)
-    second_row = jnp.stack([-proj_im, proj_re], axis=-4)
-    return jnp.stack([first_row, second_row], axis=-5)
-
-
 def solve_kernel(
-    mass_ref, source_ref, links_ref, sol_ref, res_ref,
+    mass_ref, fine_ref, proj_ref, far_links_ref, sol_ref, res_ref,
+    fine_buf, raw, wide, spread, blocks, pbuf, chain_send, chain_recv, total_buf, links_ref,
     r_buf, w_buf, halo, q_buf, p_buf, row_send, row_recv, col_send, col_recv, out_send, out_recv,
-    src_ss, src_rs, halo_ss, halo_rs, row_ss, row_rs, col_ss, col_rs, out_ss, out_rs,
+    links_ss, links_rs, fine_ls, fine_ss, fine_rs, raw_ls, raw_ss, raw_rs, blk_ss, blk_rs,
+    chain_ss, chain_rs, src_ss, src_rs,
+    halo_ss, halo_rs, row_ss, row_rs, col_ss, col_rs, out_ss, out_rs,
 ):
-    sites, full, rhs = source_ref.shape
+    sites, full, rhs = sol_ref.shape
     comps = full // 2
     part = sites // CHUNKS
     g, y, x, core = (lax.axis_index(name) for name in ALL)
@@ -82,8 +66,150 @@
         copy.start()
         pending.append(copy)
 
-    for c in range(CHUNKS):
-        start(remote(source_ref.at[chunk(c)], r_buf.at[0, chunk(c)], src_ss.at[c], src_rs.at[c], to_slot))
+    start(remote(far_links_ref, links_ref, links_ss, links_rs, to_slot))
+    for dy, peer in enumerate(col_peers):
+        rows = pl.ds(pl.multiple_of(rem(y + 1 + dy, YC) * 16, 16), 16)
+        start(remote(proj_ref.at[rows], raw.at[y], raw_ss.at[dy], raw_rs.at[dy], peer))
+    own_raw = pltpu.make_async_copy(proj_ref.at[pl.ds(pl.multiple_of(y * 16, 16), 16)], raw.at[y], raw_ls)
+    own_raw.start()
+    own_fine = []
+    for reim in range(2):
+        for h in range(2):
+            i = 2 * reim + h
+            rows = pl.ds(pl.multiple_of(reim * comps + core * FK, FK), FK)
+            start(
+                remote(
+                    fine_ref.at[:, core, :, reim, h], fine_buf.at[:, :, h, rows], fine_ss.at[i], fine_rs.at[i], mate
+                )
+            )
+            copy = pltpu.make_async_copy(
+                fine_ref.at[:, 1 - core, :, reim, h], fine_buf.at[:, :, h, rows], fine_ls.at[i]
+            )
+            copy.start()
+            own_fine.append(copy)
+
+    own_raw.wait()
+    for dy in range(YC - 1):
+        remote(proj_ref.at[pl.ds(0, 16)], raw.at[y], raw_ss.at[dy], raw_rs.at[dy], mate).wait_recv()
+    tiles = wide.shape[0]
+    for t in range(tiles):
+        for yp in range(YC):
+            wide[t, 16 * yp:16 * yp + 16] = raw[yp, :, 128 * t:128 * (t + 1)].astype(F32)
+    lanes = lax.broadcasted_iota(jnp.int32, (XC * YC, 128), 1)
+
+    def spread_group(group, carry):
+        for v in range(8):
+            acc = jnp.zeros((XC * YC, 128), F32)
+            for c in range(CORES):
+                held = {}
+                for reim in range(2):
+                    first = 2 * FK * v + FK * reim
+                    to = 2 * FK * reim + FK * c
+                    left = FK
+                    while left:
+                        tile, off = first // 128, first % 128
+                        size = min(left, 128 - off)
+                        if tile not in held:
+                            held[tile] = wide[3 * group + tile, pl.ds(c, XC * YC, stride=CORES), :]
+                        moved = pltpu.roll(held[tile], (to - off) % 128, 1) if to != off else held[tile]
+                        acc = jnp.where((lanes >= to) & (lanes < to + size), moved, acc)
+                        first, to, left = first + size, to + size, left - size
+            spread[pl.ds(8 * group + v, XC * YC, stride=comps), :] = acc
+        return carry
+
+    lax.fori_loop(0, comps // 8, spread_group, 0)
+    for xc in range(XC):
+        for yp in range(YC):
+            base = (yp * XC + xc) * comps
+            blocks[xc, yp] = spread[base:base + comps].astype(BF16)
+    owner = 1 - div(x, HALF)
+    home_slot = rem(XC - z_home, XC)
+    for i, step in enumerate((4, 3, 5, 2, 6, 1, 7, 0)):
+        xc = rem(home_slot + step, XC)
+        here = jnp.logical_and(xc == x, owner == core)
+        copy = remote(blocks.at[xc], pbuf.at[z_home], blk_ss.at[i], blk_rs.at[z_home], (g, y, xc, owner))
+
+        @pl.when(here)
+        def _():
+            pbuf[z_home] = blocks[xc]
+
+        @pl.when(jnp.logical_not(here))
+        def _():
+            copy.start()
+
+    def product(z, yp):
+        lhs = pbuf[z, yp]
+        outs = []
+        for h in range(2):
+            left = fine_buf[yp, z, h]
+            right = jnp.concatenate([left[comps:], -left[:comps]], axis=0)
+            out = jnp.dot(
+                lhs[16 * h:16 * h + 32, :full], jnp.concatenate([left, right], axis=1),
+                preferred_element_type=F32,
+            )
+            outs.append(out[8 * h:8 * h + FK])
+        return jnp.concatenate([part_[:, :rhs] for part_ in outs] + [part_[:, rhs:] for part_ in outs], axis=0)
+
+    def wait_blocks(z):
+        mine = jnp.logical_and(z == z_home, owner == core)
+
+        @pl.when(jnp.logical_not(mine))
+        def _():
+            remote(blocks.at[0], pbuf.at[z], blk_ss.at[0], blk_rs.at[z], mate).wait_recv()
+
+    for copy in own_fine:
+        copy.wait()
+    for i in range(4):
+        remote(
+            fine_ref.at[:, 0, :, 0, 0], fine_buf.at[:, :, 0, pl.ds(0, FK)], fine_ss.at[i], fine_rs.at[i], mate
+        ).wait_recv()
+
+    ways = ((1, (g, y, rem(x + 1, XC), core)), (0, (g, y, rem(x + XC - 1, XC), core)))
+    steps = (4, 3, 3, 2, 2, 1, 1)
+    for m, d in enumerate(steps):
+        for way, (plus, peer) in enumerate(ways):
+            dest = rem(x + (d if plus else XC - d), XC)
+            z = rem(XC - dest, XC)
+            if (m == 0 and way == 0) or m in (1, 3, 5):
+                wait_blocks(z)
+            if m >= 2:
+                remote(
+                    chain_send.at[way, m - 2], chain_recv.at[way, m - 2],
+                    chain_ss.at[way, m - 2], chain_rs.at[way, m - 2], mate,
+                ).wait_recv()
+            upper_half = (m + 1 - plus) % 2
+
+            def body(i, carry):
+                value = product(z, upper_half * 4 + i)
+                if m >= 2:
+                    value = value + chain_recv[way, m - 2, i]
+                chain_send[way, m, i] = value
+                return carry
+
+            lax.fori_loop(0, YC // 2, body, 0)
+            start(
+                remote(
+                    chain_send.at[way, m], chain_recv.at[way, m], chain_ss.at[way, m], chain_rs.at[way, m], peer
+                )
+            )
+    z = rem(XC - x, XC)
+    wait_blocks(z)
+    for way in range(2):
+        for m in (5, 6):
+            remote(
+                chain_send.at[way, m], chain_recv.at[way, m], chain_ss.at[way, m], chain_rs.at[way, m], mate
+            ).wait_recv()
+    for dy in (4, 3, 5, 2, 6, 1, 7, 0):
+        yp = rem(y + dy, YC)
+        high, i = div(yp, YC // 2), rem(yp, YC // 2)
+        value = product(z, yp) + chain_recv[0, 6 - high, i] + chain_recv[1, 5 + high, i]
+        if dy == 0:
+            r_buf[0, y] = value
+        else:
+            total_buf[dy] = value
+            start(
+                remote(total_buf.at[dy], r_buf.at[0, y], src_ss.at[dy - 1], src_rs.at[dy - 1], (g, yp, x, core))
+            )
 
     def send_halo(k, c):
         src = w_buf.at[k, chunk(c)]
@@ -206,11 +332,15 @@
             im = im - (c_re * e_im + c_im * e_re)
         return re, im
 
+    for dy in range(1, YC):
+        remote(
+            total_buf.at[dy], r_buf.at[0, rem(y + YC - dy, YC)], src_ss.at[dy - 1], src_rs.at[dy - 1], mate
+        ).wait_recv()
     for c in range(CHUNKS):
-        remote(source_ref.at[chunk(c)], r_buf.at[0, chunk(c)], src_ss.at[c], src_rs.at[c], mate).wait_recv()
         for s in range(c * part, (c + 1) * part):
             w_buf[0, s] = r_buf[0, s].astype(BF16)
         send_halo(0, c)
+    remote(far_links_ref, links_ref, links_ss, links_rs, mate).wait_recv()
 
     gram = {}
     alphas = []
@@ -305,22 +435,43 @@
                 target[s] = out_recv[which, s].astype(F32)
     for copy in pending:
         copy.wait_send()
-
-
-def solve(source, links, mass):
-    sites, full, rhs = source.shape
+    for i, step in enumerate((4, 3, 5, 2, 6, 1, 7, 0)):
+        xc = rem(home_slot + step, XC)
+
+        @pl.when(jnp.logical_not(jnp.logical_and(xc == x, owner == core)))
+        def _():
+            remote(blocks.at[xc], pbuf.at[z_home], blk_ss.at[i], blk_rs.at[z_home], mate).wait_send()
+
+
+def shards(fine_source, projectors, stencil_links, quark_mass):
+    sites, comps, width = stencil_links.shape[1:]
+    rhs = fine_source.shape[-1]
+    full = 2 * comps
+    columns, row = projectors.shape[1:]
+    fine = fine_source.reshape(YC, 2, XC, 2, 2, FK, rhs)
     vector = (sites, full, rhs)
     most = 3 + 4 * (ITERS - 1)
     rows = -(-most // 8) * 8
     peers_x, peers_y = XC * CORES - 1, YC - 1
     dma = pltpu.SemaphoreType.DMA
     vmem = pl.BlockSpec(memory_space=pltpu.VMEM)
-    return pl.pallas_call(
+    hbm = pl.BlockSpec(memory_space=pltpu.HBM)
+    solution, residual = pl.pallas_call(
         solve_kernel,
         out_shape=(jax.ShapeDtypeStruct(vector, F32), jax.ShapeDtypeStruct(vector, F32)),
-        in_specs=[pl.BlockSpec(memory_space=pltpu.SMEM), vmem, vmem],
+        in_specs=[pl.BlockSpec(memory_space=pltpu.SMEM), hbm, hbm, hbm],
         out_specs=(vmem, vmem),
         scratch_shapes=[
+            pltpu.VMEM((YC, XC, 2, full, rhs), BF16),
+            pltpu.VMEM((YC, columns // YC, row), BF16),
+            pltpu.VMEM((row // 128, columns, 128), F32),
+            pltpu.VMEM((XC * YC * comps, 128), F32),
+            pltpu.VMEM((XC, YC, comps, 128), BF16),
+            pltpu.VMEM((XC, YC, comps, 128), BF16),
+            pltpu.VMEM((2, 7, YC // 2, full, rhs), F32),
+            pltpu.VMEM((2, 7, YC // 2, full, rhs), F32),
+            pltpu.VMEM((YC, full, rhs), F32),
+            pltpu.VMEM((sites, comps, width), BF16),
             pltpu.VMEM((ITERS,) + vector, F32),
             pltpu.VMEM((ITERS,) + vector, BF16),
             pltpu.VMEM((ITERS, 4) + vector, BF16),
@@ -332,42 +483,22 @@
             pltpu.VMEM((ITERS, peers_y, rows, rhs), F32),
             pltpu.VMEM((2,) + vector, BF16),
             pltpu.VMEM((2,) + vector, BF16),
-            dma((CHUNKS,)), dma((CHUNKS,)),
+            dma(()), dma(()),
+            dma((4,)), dma((4,)), dma((4,)),
+            dma(()), dma((peers_y,)), dma((peers_y,)),
+            dma((XC,)), dma((XC,)),
+            dma((2, 7)), dma((2, 7)),
+            dma((peers_y,)), dma((peers_y,)),
             dma((ITERS, 4, CHUNKS)), dma((ITERS, 4, CHUNKS)),
             dma((ITERS, peers_x)), dma((ITERS, peers_x)),
             dma((ITERS, peers_y)), dma((ITERS, peers_y)),
             dma((2, CHUNKS)), dma((2, CHUNKS)),
         ],
         compiler_params=pltpu.CompilerParams(
-            collective_id=0, has_side_effects=True, vmem_limit_bytes=48 * 1024 * 1024
+            collective_id=0, has_side_effects=True, vmem_limit_bytes=56 * 1024 * 1024
         ),
-        name="gcr_solve",
-    )(mass, source, links)
-
-
-def shards(fine_source, projectors, stencil_links, quark_mass):
-    comp_count = stencil_links.shape[2]
-    null_count = comp_count // 2
-    site_count = stencil_links.shape[1]
-    column_count = projectors.shape[1]
-    block_count = column_count // site_count
-    fine_count = fine_source.shape[4]
-    rhs_count = fine_source.shape[5]
-    moves = [
-        (x * CORES + c, slot_of(x, c)[0] * CORES + slot_of(x, c)[1])
-        for x in range(XC) for c in range(CORES)
-    ]
-    links = lax.ppermute(stencil_links[0], ("x", "core"), moves)
-    regrouped = lax.all_to_all(fine_source, GROUP, split_axis=0, concat_axis=1, tiled=True)
-    fine_local = regrouped.reshape(site_count, block_count, 2, 2, fine_count, rhs_count)
-    weights = real_weights(
-        projectors.reshape(site_count, block_count, 2, null_count, 2, fine_count)
-    )
-    source = jnp.einsum(
-        "sodchvk,sochkr->sdhvr", weights, fine_local, preferred_element_type=jnp.float32
-    )
-    source = source.reshape(site_count, 2 * comp_count, rhs_count)
-    solution, residual = solve(source, links, quark_mass)
+        name="restrict_and_solve",
+    )(quark_mass, fine, projectors[0], stencil_links[0])
     return solution[None], residual[None]
 
 

time: 206 us -> 169 us (0.82)
  Pallas kernels: 93.6 us -> 164 us
  waiting for transfers between devices: 54.8 us -> 0 us
  starting transfers between devices: 29.1 us -> 0 us
  local copies, waits for them, and re-layouts: 15.7 us -> 3.54 us
  matrix products: 7.1 us -> 0 us
  other arithmetic: 3.65 us -> 0 us
    pallas_call x1, Pallas kernels: 93.6 us -> 164 us  [shards(): pl.pallas_call(solve_kernel, out_shape=(jax.ShapeDtypeStruct(vector, F32)...]
    all_to_all x1 -> x0, waiting for transfers between devices: 53.8 us -> none  [shards(): lax.all_to_all(fine_source, GROUP, split_axis=0, concat_axis=1, tiled=True)]
    all_to_all x1 -> x0, starting transfers between devices: 27.7 us -> none  [shards(): lax.all_to_all(fine_source, GROUP, split_axis=0, concat_axis=1, tiled=True)]
    slice x1 -> x0, local copies, waits for them, and re-layouts: 7.57 us -> none  [real_weights(): proj_im = proj_view[..., 1, :]]
    dot_general x1 -> x0, matrix products: 7.1 us -> none  [shards(): jnp.einsum('sodchvk,sochkr->sdhvr', weights, fine_local, preferred_elemen...]
    reshape x1 -> x0, local copies, waits for them, and re-layouts: 6.21 us -> none  [shards(): projectors.reshape(site_count, block_count, 2, null_count, 2, fine_count)]
    another operation x1 -> x0, other arithmetic: 3.24 us -> none  [real_weights(): return jnp.stack([first_row, second_row], axis=-5)]
  transfers between devices with their start and end apart: 2 -> 0, of which waited for: 2 -> 0; matrix products, arithmetic and copies ran while one was open for 12% -> 0% of each run, Pallas kernels for 0% -> 0%
where the time goes in v2:
time: 169 us; the launch traced here: 168 us
  Pallas kernels  164 us (97%)
  local copies, waits for them, and re-layouts  3.54 us (2%)
    pallas_call x1, Pallas kernels, shards(): pl.pallas_call(solve_kernel, out_shape=(jax.ShapeDtypeStruct(vector, F32)...  164 us
    unnamed x2, local copies, waits for them, and re-layouts  3.54 us

profile of v2, /device:TPU:517, one launch (start us, length us, event | category | flops | bytes accessed | tf_op | source)
XLA Modules:
  0.0 168.4 jit_solution(229831295933861327)
XLA Ops:
  1.3 163.6 %restrict_and_solve.1 = (f32[8,96,128]{2,1,0:T(8,128)}, f32[8,96,128]{2,1,0:T(8,128)}) custom-call(f32[1]{0:T(128)S(6)} %copy.8.mass_ref, bf16[8,2,8,2,2,24,128]{6,5,4,3,2,1,0:T(8,128)(2,1)} %bitcast.5, bf16[128,2304]{1,0:T(8,128)(2,1)} %bitcast.7, bf16[8,48,864]{2,1,0:T(8,128)(2,1)} %bitcast.6), custom_call_target="tpu_custom_call" | custom-call | tf_op jit(solution)/shard_map/restrict_and_solve/pallas_call | solution.py:459
  164.8 1.8 %copy.9 = f32[1,8,96,128]{3,2,1,0:T(8,128)} copy(f32[1,8,96,128]{3,2,1,0:T(8,128)} %bitcast.9) | data formatting | bytes 786432
  166.6 1.8 %copy.10 = f32[1,8,96,128]{3,2,1,0:T(8,128)} copy(f32[1,8,96,128]{3,2,1,0:T(8,128)} %bitcast.8) | data formatting | bytes 786432

commit v3 on v1

--- a/solution.py
+++ b/solution.py
@@ -1,5 +1,3 @@
-import functools
-
 import jax
 import jax.numpy as jnp
 from jax import lax
@@ -16,41 +14,55 @@
 ALL = ("cfg", "y", "x", "core")
 MESH = pl.DeviceIdType.MESH
 CHUNKS = 2
+EARLY = 5
+FK = 24
+PACKED = 40
+ORDER = (
+    ((0, 4), (1, 4), (2, 3), (0, 3), (1, 3), (3, 3), (0, 2), (1, 2), (2, 2), (0, 1), (1, 1), (3, 2), (2, 1), (3, 1)),
+    ((0, 3), (1, 3), (2, 4), (3, 4), (0, 2), (1, 2), (2, 3), (3, 3), (0, 1), (1, 1), (2, 2), (3, 2), (2, 1), (3, 1)),
+)
 F32, BF16 = jnp.float32, jnp.bfloat16
 
 
-def slot_of(x, core):
-    z = 2 * (x % HALF) + core
-    return (XC - z) % XC, 1 - x // HALF
-
-
-def home_of(x, core):
-    z = (XC - x) % XC
-    return HALF * (1 - core) + z // 2, z % 2
-
-
-def real_weights(proj_view):
-    proj_re = proj_view[..., 0, :]
-    proj_im = proj_view[..., 1, :]
-    first_row = jnp.stack([proj_re, proj_im], axis=-4)
-    second_row = jnp.stack([-proj_im, proj_re], axis=-4)
-    return jnp.stack([first_row, second_row], axis=-5)
+def remote(src, dst, send_sem, recv_sem, peer):
+    return pltpu.make_async_remote_copy(
+        src_ref=src, dst_ref=dst, send_sem=send_sem, recv_sem=recv_sem,
+        device_id=peer, device_id_type=MESH,
+    )
+
+
+def places():
+    g, y, x, core = (lax.axis_index(name) for name in ALL)
+    z_home = 2 * lax.rem(x, HALF) + core
+    z_slot = lax.rem(XC - x, XC)
+    to_slot = (g, y, lax.rem(XC - z_home, XC), 1 - lax.div(x, HALF))
+    to_home = (g, y, HALF * (1 - core) + lax.div(z_slot, 2), lax.rem(z_slot, 2))
+    return g, y, x, core, z_home, z_slot, to_slot, to_home
+
+
+def meet(peers):
+    barrier = pltpu.get_barrier_semaphore()
+    for peer in peers:
+        pl.semaphore_signal(barrier, inc=1, device_id=peer, device_id_type=MESH)
+
+
+def met(peers):
+    pl.semaphore_wait(pltpu.get_barrier_semaphore(), len(peers))
 
 
 def solve_kernel(
-    mass_ref, source_ref, links_ref, sol_ref, res_ref,
-    r_buf, w_buf, halo, q_buf, p_buf, row_send, row_recv, col_send, col_recv, out_send, out_recv,
-    src_ss, src_rs, halo_ss, halo_rs, row_ss, row_rs, col_ss, col_rs, out_ss, out_rs,
+    mass_ref, fine_ref, proj_ref, far_links_ref, out_recv,
+    fine_buf, raw, wide, spread, blocks, packed, pbuf, chain_send, chain_recv, total_buf, links_ref,
+    r_buf, w_buf, halo, q_buf, w_home, row_send, row_recv, col_send, col_recv, out_send,
+    links_ss, links_rs, fine_ls, fine_ss, fine_rs, raw_ls, raw_ss, raw_rs, blk_ss, blk_rs,
+    chain_ss, chain_rs, src_ss, src_rs,
+    halo_ss, halo_rs, row_ss, row_rs, col_ss, col_rs, home_ss, home_rs, out_ss, out_rs,
 ):
-    sites, full, rhs = source_ref.shape
+    sites, full, rhs = out_recv.shape[1:]
     comps = full // 2
     part = sites // CHUNKS
-    g, y, x, core = (lax.axis_index(name) for name in ALL)
     rem, div = lax.rem, lax.div
-    z_home = 2 * rem(x, HALF) + core
-    to_slot = (g, y, rem(XC - z_home, XC), 1 - div(x, HALF))
-    z_slot = rem(XC - x, XC)
-    to_home = (g, y, HALF * (1 - core) + div(z_slot, 2), rem(z_slot, 2))
+    g, y, x, core, z_home, z_slot, to_slot, to_home = places()
     odd = 1 - core
     upper = (g, y, rem(x + XC - 1, XC), core)
     lower = (g, y, rem(x + 1, XC), core)
@@ -61,17 +73,8 @@
     ]
     col_peers = [(g, rem(y + d, YC), x, core) for d in range(1, YC)]
 
-    barrier = pltpu.get_barrier_semaphore()
     everyone = row_peers + col_peers + [beyond]
-    for peer in everyone:
-        pl.semaphore_signal(barrier, inc=1, device_id=peer, device_id_type=MESH)
-    pl.semaphore_wait(barrier, len(everyone))
-
-    def remote(src, dst, send_sem, recv_sem, peer):
-        return pltpu.make_async_remote_copy(
-            src_ref=src, dst_ref=dst, send_sem=send_sem, recv_sem=recv_sem,
-            device_id=peer, device_id_type=MESH,
-        )
+    meet(everyone)
 
     def chunk(c):
         return pl.ds(c * part, part)
@@ -81,9 +84,6 @@
     def start(copy):
         copy.start()
         pending.append(copy)
-
-    for c in range(CHUNKS):
-        start(remote(source_ref.at[chunk(c)], r_buf.at[0, chunk(c)], src_ss.at[c], src_rs.at[c], to_slot))
 
     def send_halo(k, c):
         src = w_buf.at[k, chunk(c)]
@@ -191,6 +191,7 @@
             start(
                 remote(col_send.at[k, rows], col_recv.at[k, d, rows], col_ss.at[k, d], col_rs.at[k, d], peer)
             )
+        start(remote(w_buf.at[k], w_home.at[k], home_ss.at[k], home_rs.at[k], to_home))
         for d in range(len(col_peers)):
             remote(
                 col_send.at[k, rows], col_recv.at[k, d, rows], col_ss.at[k, d], col_rs.at[k, d], mate
@@ -206,15 +207,208 @@
             im = im - (c_re * e_im + c_im * e_re)
         return re, im
 
+    columns = raw.shape[1]
+    columns = raw.shape[1]
+    own_raw = pltpu.make_async_copy(
+        proj_ref.at[pl.ds(pl.multiple_of(y * columns, columns), columns)], raw.at[y], raw_ls
+    )
+    own_fine = []
+    for reim in range(2):
+        for h in range(2):
+            i = 2 * reim + h
+            rows = pl.ds(pl.multiple_of(reim * comps + core * FK, FK), FK)
+            own_fine.append(
+                pltpu.make_async_copy(
+                    fine_ref.at[:, 1 - core, :, reim, h], fine_buf.at[:, :, h, rows], fine_ls.at[i]
+                )
+            )
+    for copy in [own_raw] + own_fine:
+        copy.start()
+
+    def links_copy(c):
+        span_ = (pl.ds(0, EARLY), pl.ds(EARLY, sites - EARLY))[c]
+        return remote(far_links_ref.at[span_], links_ref.at[span_], links_ss.at[c], links_rs.at[c], to_slot)
+
+    met(everyone)
+    for dy, peer in enumerate(col_peers):
+        rows = pl.ds(pl.multiple_of(rem(y + 1 + dy, YC) * columns, columns), columns)
+        start(remote(proj_ref.at[rows], raw.at[y], raw_ss.at[dy], raw_rs.at[dy], peer))
+    start(links_copy(0))
+    for reim in range(2):
+        for h in range(2):
+            i = 2 * reim + h
+            rows = pl.ds(pl.multiple_of(reim * comps + core * FK, FK), FK)
+            start(
+                remote(
+                    fine_ref.at[:, core, :, reim, h], fine_buf.at[:, :, h, rows], fine_ss.at[i], fine_rs.at[i], mate
+                )
+            )
+
+    own_raw.wait()
+    for dy in range(YC - 1):
+        remote(proj_ref.at[pl.ds(0, columns)], raw.at[y], raw_ss.at[dy], raw_rs.at[dy], mate).wait_recv()
+    tiles = wide.shape[0]
+    for t in range(tiles):
+        for yp in range(YC):
+            wide[t, 16 * yp:16 * yp + 16] = raw[yp, :, 128 * t:128 * (t + 1)].astype(F32)
+    lanes = lax.broadcasted_iota(jnp.int32, (XC * YC, 128), 1)
+
+    def spread_group(group, carry):
+        for v in range(8):
+            acc = jnp.zeros((XC * YC, 128), F32)
+            for c in range(CORES):
+                held = {}
+                for reim in range(2):
+                    first = 2 * FK * v + FK * reim
+                    to = 2 * FK * reim + FK * c
+                    left = FK
+                    while left:
+                        tile, off = first // 128, first % 128
+                        size = min(left, 128 - off)
+                        if tile not in held:
+                            held[tile] = wide[3 * group + tile, pl.ds(c, XC * YC, stride=CORES), :]
+                        moved = pltpu.roll(held[tile], (to - off) % 128, 1) if to != off else held[tile]
+                        acc = jnp.where((lanes >= to) & (lanes < to + size), moved, acc)
+                        first, to, left = first + size, to + size, left - size
+            spread[pl.ds(8 * group + v, XC * YC, stride=comps), :] = acc
+        return carry
+
+    lax.fori_loop(0, comps // 8, spread_group, 0)
+    lane = lax.broadcasted_iota(jnp.int32, (8, 128), 1)
+    low_lanes = lane < full
+    for xc in range(XC):
+        for yp in range(YC):
+            base = (yp * XC + xc) * comps
+            tail = spread[base + PACKED:base + comps]
+            head = [
+                jnp.where(low_lanes, spread[base + 8 * j:base + 8 * j + 8], pltpu.roll(tail, full - 32 * j, 1))
+                for j in range(3)
+            ]
+            blocks[xc, yp] = jnp.concatenate(head + [spread[base + 24:base + PACKED]], axis=0).astype(BF16)
+    owner = 1 - div(x, HALF)
+    home_slot = rem(XC - z_home, XC)
+    for i, step in enumerate((4, 3, 5, 2, 6, 1, 7, 0)):
+        xc = rem(home_slot + step, XC)
+        here = jnp.logical_and(xc == x, owner == core)
+        copy = remote(blocks.at[xc], packed.at[z_home], blk_ss.at[i], blk_rs.at[z_home], (g, y, xc, owner))
+
+        @pl.when(here)
+        def _():
+            packed[z_home] = blocks[xc]
+
+        @pl.when(jnp.logical_not(here))
+        def _():
+            copy.start()
+
+    def product(z, yp):
+        lhs = pbuf[z, yp]
+        outs = []
+        for h in range(2):
+            left = fine_buf[yp, z, h]
+            right = jnp.concatenate([left[comps:], -left[:comps]], axis=0)
+            out = jnp.dot(
+                lhs[16 * h:16 * h + 32, :full], jnp.concatenate([left, right], axis=1),
+                preferred_element_type=F32,
+            )
+            outs.append(out[8 * h:8 * h + FK])
+        return jnp.concatenate([part_[:, :rhs] for part_ in outs] + [part_[:, rhs:] for part_ in outs], axis=0)
+
+    def wait_blocks(z):
+        mine = jnp.logical_and(z == z_home, owner == core)
+
+        @pl.when(jnp.logical_not(mine))
+        def _():
+            remote(blocks.at[0], packed.at[z], blk_ss.at[0], blk_rs.at[z], mate).wait_recv()
+
+        def unpack(yp, carry):
+            held = packed[z, yp]
+            rows = held[0:24].astype(F32)
+            moved = [pltpu.roll(rows[8 * j:8 * j + 8], 32 * (j + 1), 1) for j in range(3)]
+            tail = jnp.where(lane < 32, moved[0], jnp.where(lane < 64, moved[1], moved[2]))
+            pbuf[z, yp] = jnp.concatenate([held.astype(F32), tail], axis=0).astype(BF16)
+            return carry
+
+        lax.fori_loop(0, YC, unpack, 0)
+
+    for copy in own_fine:
+        copy.wait()
+    for i in range(4):
+        remote(
+            fine_ref.at[:, 0, :, 0, 0], fine_buf.at[:, :, 0, pl.ds(0, FK)], fine_ss.at[i], fine_rs.at[i], mate
+        ).wait_recv()
+
+    ways = ((1, (g, y, rem(x + 1, XC), core)), (0, (g, y, rem(x + XC - 1, XC), core)))
+    waited = set()
+
+    def received(way, m):
+        remote(
+            chain_send.at[way, m], chain_recv.at[way, m], chain_ss.at[way, m], chain_rs.at[way, m], mate
+        ).wait_recv()
+
+    def finish(quarter):
+        z = z_slot
+        if 0 not in waited:
+            waited.add(0)
+            wait_blocks(z)
+        last = [ORDER[way].index((quarter, 1)) for way in range(2)]
+        for way in range(2):
+            received(way, last[way])
+        for i in range(2):
+            yp = 2 * quarter + i
+            total_buf[yp] = product(z, yp) + chain_recv[0, last[0], i] + chain_recv[1, last[1], i]
+
+            @pl.when(y == yp)
+            def _():
+                r_buf[0, yp] = total_buf[yp]
+
+            @pl.when(y != yp)
+            def _():
+                remote(total_buf.at[yp], r_buf.at[0, y], src_ss.at[yp], src_rs.at[y], (g, yp, x, core)).start()
+
+    for m in range(len(ORDER[0])):
+        for way, (plus, peer) in enumerate(ways):
+            quarter, d = ORDER[way][m]
+            sign = d if plus else -d
+            z = rem(XC - rem(x + XC + sign, XC), XC)
+            key = sign % XC
+            if key not in waited:
+                waited.add(key)
+                wait_blocks(z)
+            before = (quarter, d + 1)
+            source = ORDER[way].index(before) if before in ORDER[way] else None
+            if source is not None:
+                received(way, source)
+            for i in range(2):
+                value = product(z, 2 * quarter + i)
+                if source is not None:
+                    value = value + chain_recv[way, source, i]
+                chain_send[way, m, i] = value
+            start(
+                remote(
+                    chain_send.at[way, m], chain_recv.at[way, m], chain_ss.at[way, m], chain_rs.at[way, m], peer
+                )
+            )
+        if m in (11, 12):
+            finish(m - 11)
+    start(links_copy(1))
+    finish(2)
+    finish(3)
+    for s in range(sites):
+
+        @pl.when(y != s)
+        def _():
+            remote(total_buf.at[s], r_buf.at[0, s], src_ss.at[s], src_rs.at[s], mate).wait_recv()
+
     for c in range(CHUNKS):
-        remote(source_ref.at[chunk(c)], r_buf.at[0, chunk(c)], src_ss.at[c], src_rs.at[c], mate).wait_recv()
         for s in range(c * part, (c + 1) * part):
             w_buf[0, s] = r_buf[0, s].astype(BF16)
         send_halo(0, c)
+    for c in range(CHUNKS):
+        links_copy(c).wait_recv()
 
     gram = {}
-    alphas = []
-    factors = []
+    basis = []
+    betas = []
     for k in range(ITERS):
         totals = all_reduce(k, matvec(k))
         squared, a_re, a_im = totals[:3]
@@ -242,8 +436,6 @@
                 lack_im = (1.0 - gram[j, j][0]) * c_im
                 gram[j, k] = (factor * lack_re, factor * lack_im)
         a_re, a_im = a_re * factor, a_im * factor
-        alphas.append((a_re, a_im))
-        factors.append(factor)
         last = k + 1 == ITERS
         for c in range(CHUNKS):
             for s in range(c * part, (c + 1) * part):
@@ -253,8 +445,8 @@
                 r_re = r_re - (a_re * q_re - a_im * q_im)
                 r_im = r_im - (a_re * q_im + a_im * q_re)
                 if last:
-                    out_send[1, s, 0:comps] = r_re.astype(BF16)
-                    out_send[1, s, comps:full] = r_im.astype(BF16)
+                    out_send[s, 0:comps] = r_re.astype(BF16)
+                    out_send[s, comps:full] = r_im.astype(BF16)
                 else:
                     q_buf[k, s, 0:comps] = q_re
                     q_buf[k, s, comps:full] = q_im
@@ -264,111 +456,109 @@
                     w_buf[k + 1, s, comps:full] = r_im.astype(BF16)
             if last:
                 start(
-                    remote(
-                        out_send.at[1, chunk(c)], out_recv.at[1, chunk(c)], out_ss.at[1, c], out_rs.at[1, c],
-                        to_home,
-                    )
+                    remote(out_send.at[chunk(c)], out_recv.at[1, chunk(c)], out_ss.at[c], out_rs.at[c], to_home)
                 )
             else:
                 send_halo(k + 1, c)
-        for c in range(CHUNKS):
-            for s in range(c * part, (c + 1) * part):
-                p_re, p_im = minus(r_buf[k, s], coefs, p_buf, s)
-                p_re, p_im = p_re * factor, p_im * factor
-                if last:
-                    s_re = a_re * p_re - a_im * p_im
-                    s_im = a_re * p_im + a_im * p_re
-                    for j in range(k):
-                        e_re, e_im = split(p_buf[j, s])
-                        b_re, b_im = alphas[j]
-                        s_re = s_re + (b_re * e_re - b_im * e_im)
-                        s_im = s_im + (b_re * e_im + b_im * e_re)
-                    out_send[0, s, 0:comps] = s_re.astype(BF16)
-                    out_send[0, s, comps:full] = s_im.astype(BF16)
-                else:
-                    p_buf[k, s, 0:comps] = p_re
-                    p_buf[k, s, comps:full] = p_im
-            if last:
-                start(
-                    remote(
-                        out_send.at[0, chunk(c)], out_recv.at[0, chunk(c)], out_ss.at[0, c], out_rs.at[0, c],
-                        to_home,
-                    )
-                )
-    for which, target in ((1, res_ref), (0, sol_ref)):
-        for c in range(CHUNKS):
-            remote(
-                out_send.at[which, chunk(c)], out_recv.at[which, chunk(c)],
-                out_ss.at[which, c], out_rs.at[which, c], mate,
-            ).wait_recv()
-            for s in range(c * part, (c + 1) * part):
-                target[s] = out_recv[which, s].astype(F32)
+        row = [(0.0, 0.0)] * k + [(factor, 0.0)]
+        for j, (c_re, c_im) in enumerate(coefs):
+            f_re, f_im = factor * c_re, factor * c_im
+            for i in range(j + 1):
+                u_re, u_im = basis[j][i]
+                row[i] = (row[i][0] - (f_re * u_re - f_im * u_im), row[i][1] - (f_re * u_im + f_im * u_re))
+        basis.append(row)
+        for i in range(k + 1):
+            u_re, u_im = row[i]
+            b_re, b_im = betas[i] if i < len(betas) else (0.0, 0.0)
+            term = (b_re + a_re * u_re - a_im * u_im, b_im + a_re * u_im + a_im * u_re)
+            betas[i:i + 1] = [term]
+    for k in range(ITERS):
+        remote(w_buf.at[k], w_home.at[k], home_ss.at[k], home_rs.at[k], mate).wait_recv()
+    for s in range(sites):
+        s_re = s_im = 0.0
+        for k in range(ITERS):
+            b_re, b_im = betas[k]
+            e_re, e_im = split(w_home[k, s].astype(F32))
+            s_re = s_re + (b_re * e_re - b_im * e_im)
+            s_im = s_im + (b_re * e_im + b_im * e_re)
+        out_recv[0, s, 0:comps] = s_re.astype(BF16)
+        out_recv[0, s, comps:full] = s_im.astype(BF16)
+    for c in range(CHUNKS):
+        remote(out_send.at[chunk(c)], out_recv.at[1, chunk(c)], out_ss.at[c], out_rs.at[c], mate).wait_recv()
     for copy in pending:
         copy.wait_send()
-
-
-def solve(source, links, mass):
-    sites, full, rhs = source.shape
+    for i, step in enumerate((4, 3, 5, 2, 6, 1, 7, 0)):
+        xc = rem(home_slot + step, XC)
+
+        @pl.when(jnp.logical_not(jnp.logical_and(xc == x, owner == core)))
+        def _():
+            remote(blocks.at[xc], packed.at[z_home], blk_ss.at[i], blk_rs.at[z_home], mate).wait_send()
+
+    for yp in range(YC):
+
+        @pl.when(y != yp)
+        def _():
+            remote(total_buf.at[yp], r_buf.at[0, yp], src_ss.at[yp], src_rs.at[yp], mate).wait_send()
+
+
+def shards(fine_source, projectors, stencil_links, quark_mass):
+    sites, comps, width = stencil_links.shape[1:]
+    rhs = fine_source.shape[-1]
+    full = 2 * comps
+    columns, row = projectors.shape[1:]
+    fine = fine_source.reshape(YC, 2, XC, 2, 2, FK, rhs)
     vector = (sites, full, rhs)
     most = 3 + 4 * (ITERS - 1)
     rows = -(-most // 8) * 8
     peers_x, peers_y = XC * CORES - 1, YC - 1
     dma = pltpu.SemaphoreType.DMA
     vmem = pl.BlockSpec(memory_space=pltpu.VMEM)
-    return pl.pallas_call(
+    hbm = pl.BlockSpec(memory_space=pltpu.HBM)
+    messages = len(ORDER[0])
+    result = pl.pallas_call(
         solve_kernel,
-        out_shape=(jax.ShapeDtypeStruct(vector, F32), jax.ShapeDtypeStruct(vector, F32)),
-        in_specs=[pl.BlockSpec(memory_space=pltpu.SMEM), vmem, vmem],
-        out_specs=(vmem, vmem),
+        out_shape=jax.ShapeDtypeStruct((2,) + vector, BF16),
+        in_specs=[pl.BlockSpec(memory_space=pltpu.SMEM), hbm, hbm, hbm],
+        out_specs=vmem,
         scratch_shapes=[
+            pltpu.VMEM((YC, XC, 2, full, rhs), BF16),
+            pltpu.VMEM((YC, columns // YC, row), BF16),
+            pltpu.VMEM((row // 128, columns, 128), F32),
+            pltpu.VMEM((XC * YC * comps, 128), F32),
+            pltpu.VMEM((XC, YC, PACKED, 128), BF16),
+            pltpu.VMEM((XC, YC, PACKED, 128), BF16),
+            pltpu.VMEM((XC, YC, comps, 128), BF16),
+            pltpu.VMEM((2, messages, 2, full, rhs), F32),
+            pltpu.VMEM((2, messages, 2, full, rhs), F32),
+            pltpu.VMEM((YC, full, rhs), F32),
+            pltpu.VMEM((sites, comps, width), BF16),
             pltpu.VMEM((ITERS,) + vector, F32),
             pltpu.VMEM((ITERS,) + vector, BF16),
             pltpu.VMEM((ITERS, 4) + vector, BF16),
             pltpu.VMEM((ITERS,) + vector, F32),
-            pltpu.VMEM((ITERS - 1,) + vector, F32),
+            pltpu.VMEM((ITERS,) + vector, BF16),
             pltpu.VMEM((ITERS, rows, rhs), F32),
             pltpu.VMEM((ITERS, peers_x, rows, rhs), F32),
             pltpu.VMEM((ITERS, rows, rhs), F32),
             pltpu.VMEM((ITERS, peers_y, rows, rhs), F32),
-            pltpu.VMEM((2,) + vector, BF16),
-            pltpu.VMEM((2,) + vector, BF16),
-            dma((CHUNKS,)), dma((CHUNKS,)),
+            pltpu.VMEM(vector, BF16),
+            dma((CHUNKS,)), dma((CHUNKS,)), dma((4,)), dma((4,)), dma((4,)),
+            dma(()), dma((peers_y,)), dma((peers_y,)),
+            dma((XC,)), dma((XC,)),
+            dma((2, messages)), dma((2, messages)),
+            dma((YC,)), dma((YC,)),
             dma((ITERS, 4, CHUNKS)), dma((ITERS, 4, CHUNKS)),
             dma((ITERS, peers_x)), dma((ITERS, peers_x)),
             dma((ITERS, peers_y)), dma((ITERS, peers_y)),
-            dma((2, CHUNKS)), dma((2, CHUNKS)),
+            dma((ITERS,)), dma((ITERS,)), dma((CHUNKS,)), dma((CHUNKS,)),
         ],
         compiler_params=pltpu.CompilerParams(
-            collective_id=0, has_side_effects=True, vmem_limit_bytes=48 * 1024 * 1024
+            collective_id=0, has_side_effects=True, vmem_limit_bytes=56 * 1024 * 1024
         ),
-        name="gcr_solve",
-    )(mass, source, links)
-
-
-def shards(fine_source, projectors, stencil_links, quark_mass):
-    comp_count = stencil_links.shape[2]
-    null_count = comp_count // 2
-    site_count = stencil_links.shape[1]
-    column_count = projectors.shape[1]
-    block_count = column_count // site_count
-    fine_count = fine_source.shape[4]
-    rhs_count = fine_source.shape[5]
-    moves = [
-        (x * CORES + c, slot_of(x, c)[0] * CORES + slot_of(x, c)[1])
-        for x in range(XC) for c in range(CORES)
-    ]
-    links = lax.ppermute(stencil_links[0], ("x", "core"), moves)
-    regrouped = lax.all_to_all(fine_source, GROUP, split_axis=0, concat_axis=1, tiled=True)
-    fine_local = regrouped.reshape(site_count, block_count, 2, 2, fine_count, rhs_count)
-    weights = real_weights(
-        projectors.reshape(site_count, block_count, 2, null_count, 2, fine_count)
-    )
-    source = jnp.einsum(
-        "sodchvk,sochkr->sdhvr", weights, fine_local, preferred_element_type=jnp.float32
-    )
-    source = source.reshape(site_count, 2 * comp_count, rhs_count)
-    solution, residual = solve(source, links, quark_mass)
-    return solution[None], residual[None]
+        name="restrict_and_solve",
+    )(quark_mass, fine, projectors[0], stencil_links[0])
+    result = result.astype(F32)
+    return result[0:1], result[1:2]
 
 
 def solution(mesh):

time: 206 us -> 162 us (0.79)
  Pallas kernels: 93.6 us -> 158 us
  waiting for transfers between devices: 54.8 us -> 0 us
  starting transfers between devices: 29.1 us -> 0 us
  local copies, waits for them, and re-layouts: 15.7 us -> 1.98 us
  matrix products: 7.1 us -> 0 us
  other arithmetic: 3.65 us -> 0 us
    pallas_call x1, Pallas kernels: 93.6 us -> 158 us  [shards(): pl.pallas_call(solve_kernel, out_shape=jax.ShapeDtypeStruct((2,) + vector...]
    all_to_all x1 -> x0, waiting for transfers between devices: 53.8 us -> none  [shards(): lax.all_to_all(fine_source, GROUP, split_axis=0, concat_axis=1, tiled=True)]
    all_to_all x1 -> x0, starting transfers between devices: 27.7 us -> none  [shards(): lax.all_to_all(fine_source, GROUP, split_axis=0, concat_axis=1, tiled=True)]
    dot_general x1 -> x0, matrix products: 7.1 us -> none  [shards(): jnp.einsum('sodchvk,sochkr->sdhvr', weights, fine_local, preferred_elemen...]
    reshape x1 -> x0, local copies, waits for them, and re-layouts: 6.21 us -> none  [shards(): projectors.reshape(site_count, block_count, 2, null_count, 2, fine_count)]
    slice x1, local copies, waits for them, and re-layouts: 7.57 us -> 1.98 us  [shards(): return (result[0:1], result[1:2])]
    another operation x1 -> x0, other arithmetic: 3.24 us -> none  [real_weights(): return jnp.stack([first_row, second_row], axis=-5)]
  transfers between devices with their start and end apart: 2 -> 0, of which waited for: 2 -> 0; matrix products, arithmetic and copies ran while one was open for 12% -> 0% of each run, Pallas kernels for 0% -> 0%
where the time goes in v3:
time: 162 us; the launch traced here: 161 us
  Pallas kernels  158 us (98%)
  local copies, waits for them, and re-layouts  1.98 us (1%)
    pallas_call x1, Pallas kernels, shards(): pl.pallas_call(solve_kernel, out_shape=jax.ShapeDtypeStruct((2,) + vector...  158 us

profile of v3, /device:TPU:517, one launch (start us, length us, event | category | flops | bytes accessed | tf_op | source)
XLA Modules:
  0.0 161.4 jit_solution(17682533203124859720)
XLA Ops:
  1.3 158.2 %restrict_and_solve.1 = bf16[2,8,96,128]{3,2,1,0:T(8,128)(2,1)} custom-call(f32[1]{0:T(128)S(6)} %copy.6.mass_ref, bf16[8,2,8,2,2,24,128]{6,5,4,3,2,1,0:T(8,128)(2,1)} %bitcast.3, bf16[128,2304]{1,0:T(8,128)(2,1)} %bitcast.5, bf16[8,48,864]{2,1,0:T(8,128)(2,1)} %bitcast.4), custom_call_target="tpu_custom_call" | custom-call | tf_op jit(solution)/shard_map/restrict_and_solve/pallas_call | solution.py:518
  159.4 2.0 %fusion = (f32[1,8,96,128]{3,2,1,0:T(8,128)}, f32[1,8,96,128]{3,2,1,0:T(8,128)}) fusion(bf16[2,8,96,128]{3,2,1,0:T(8,128)(2,1)} %restrict_and_solve.1), kind=kLoop, calls=%fused_computation | loop fusion | bytes 1572864 | tf_op jit(solution)/shard_map/slice | solution.py:561

commit v4 on v3

--- a/solution.py
+++ b/solution.py
@@ -56,7 +56,7 @@
     r_buf, w_buf, halo, q_buf, w_home, row_send, row_recv, col_send, col_recv, out_send,
     links_ss, links_rs, fine_ls, fine_ss, fine_rs, raw_ls, raw_ss, raw_rs, blk_ss, blk_rs,
     chain_ss, chain_rs, src_ss, src_rs,
-    halo_ss, halo_rs, row_ss, row_rs, col_ss, col_rs, home_ss, home_rs, out_ss, out_rs,
+    first_ss, first_rs, halo_ss, halo_rs, row_ss, row_rs, col_ss, col_rs, home_ss, home_rs, out_ss, out_rs,
 ):
     sites, full, rhs = out_recv.shape[1:]
     comps = full // 2
@@ -85,18 +85,25 @@
         copy.start()
         pending.append(copy)
 
+    neighbours = ((1, upper), (0, lower), (3 - odd, mate), (2 + odd, beyond))
+
     def send_halo(k, c):
-        src = w_buf.at[k, chunk(c)]
-        for kind, peer in ((1, upper), (0, lower), (3 - odd, mate), (2 + odd, beyond)):
-            place = {0: 0, 1: 1}.get(kind, 2) if isinstance(kind, int) else (2 if peer is mate else 3)
+        for place, (kind, peer) in enumerate(neighbours):
             start(
                 remote(
-                    src, halo.at[k, kind, chunk(c)], halo_ss.at[k, place, c], halo_rs.at[k, kind, c], peer
+                    w_buf.at[k, chunk(c)], halo.at[k, kind, chunk(c)],
+                    halo_ss.at[k, place, c], halo_rs.at[k, kind, c], peer,
                 )
             )
 
     def wait_halo(k):
         for kind in range(4):
+            if k == 0:
+                for s in range(sites):
+                    remote(
+                        w_buf.at[0, s], halo.at[0, kind, s], first_ss.at[0, s], first_rs.at[kind, s], mate
+                    ).wait_recv()
+                continue
             for c in range(CHUNKS):
                 remote(
                     w_buf.at[k, chunk(c)], halo.at[k, kind, chunk(c)],
@@ -393,16 +400,13 @@
     start(links_copy(1))
     finish(2)
     finish(3)
-    for s in range(sites):
-
-        @pl.when(y != s)
-        def _():
+    for dy in (0, 1, 7, 2, 6, 3, 5, 4):
+        s = rem(y + dy, YC)
+        if dy:
             remote(total_buf.at[s], r_buf.at[0, s], src_ss.at[s], src_rs.at[s], mate).wait_recv()
-
-    for c in range(CHUNKS):
-        for s in range(c * part, (c + 1) * part):
-            w_buf[0, s] = r_buf[0, s].astype(BF16)
-        send_halo(0, c)
+        w_buf[0, s] = r_buf[0, s].astype(BF16)
+        for place, (kind, peer) in enumerate(neighbours):
+            start(remote(w_buf.at[0, s], halo.at[0, kind, s], first_ss.at[place, s], first_rs.at[kind, s], peer))
     for c in range(CHUNKS):
         links_copy(c).wait_recv()
 
@@ -547,6 +551,7 @@
             dma((XC,)), dma((XC,)),
             dma((2, messages)), dma((2, messages)),
             dma((YC,)), dma((YC,)),
+            dma((4, sites)), dma((4, sites)),
             dma((ITERS, 4, CHUNKS)), dma((ITERS, 4, CHUNKS)),
             dma((ITERS, peers_x)), dma((ITERS, peers_x)),
             dma((ITERS, peers_y)), dma((ITERS, peers_y)),

time: 162 us -> 161 us (level)
  no operation moved by 1% of the time
where the time goes in v4:
time: 161 us; the launch traced here: 160 us
  Pallas kernels  157 us (98%)
  local copies, waits for them, and re-layouts  1.98 us (1%)
    pallas_call x1, Pallas kernels, shards(): pl.pallas_call(solve_kernel, out_shape=jax.ShapeDtypeStruct((2,) + vector...  157 us

profile of v4, /device:TPU:517, one launch (start us, length us, event | category | flops | bytes accessed | tf_op | source)
XLA Modules:
  0.0 160.5 jit_solution(9956099889409677150)
XLA Ops:
  1.3 157.2 %restrict_and_solve.1 = bf16[2,8,96,128]{3,2,1,0:T(8,128)(2,1)} custom-call(f32[1]{0:T(128)S(6)} %copy.6.mass_ref, bf16[8,2,8,2,2,24,128]{6,5,4,3,2,1,0:T(8,128)(2,1)} %bitcast.3, bf16[128,2304]{1,0:T(8,128)(2,1)} %bitcast.5, bf16[8,48,864]{2,1,0:T(8,128)(2,1)} %bitcast.4), custom_call_target="tpu_custom_call" | custom-call | tf_op jit(solution)/shard_map/restrict_and_solve/pallas_call | solution.py:522
  158.5 2.0 %fusion = (f32[1,8,96,128]{3,2,1,0:T(8,128)}, f32[1,8,96,128]{3,2,1,0:T(8,128)}) fusion(bf16[2,8,96,128]{3,2,1,0:T(8,128)(2,1)} %restrict_and_solve.1), kind=kLoop, calls=%fused_computation | loop fusion | bytes 1572864 | tf_op jit(solution)/shard_map/slice | solution.py:566
